TPU v7x, 128 devices: a whole 4x4x4 slice. The times are simulated.
128 devices in a mesh: gx: 4 (over y), gy: 8 (over z_hi, x), gz: 4 (over z_lo, core).
Axes of the slice: x: 4, y: 4, z: 4 (z_hi: 2, z_lo: 2; z = z_hi * 2 + z_lo), core: 2. Of those that a mesh axis runs over, the one named last changes fastest.
Arguments:
- noisy_image: float32 [32, 256, 512], P('gz', 'gy', 'gx'), may hold values from -6 to 6
- fidelity: float32 [32, 256, 512], P('gz', 'gy', 'gx'), may hold values from 0.5 to 8
- primal_u: float32 [32, 256, 512], P('gz', 'gy', 'gx'), may hold values from -6 to 6
- primal_v: float32 [3, 32, 256, 512], P(None, 'gz', 'gy', 'gx'), may hold values from -2 to 2
- dual_p: float32 [3, 32, 256, 512], P(None, 'gz', 'gy', 'gx'), may hold values from -2.5 to 2.5
- dual_q: float32 [6, 32, 256, 512], P(None, 'gz', 'gy', 'gx'), may hold values from -2.5 to 2.5
Outputs:
- denoised: float32 [32, 256, 512], P('gz', 'gy', 'gx')
- vector_field: float32 [3, 32, 256, 512], P(None, 'gz', 'gy', 'gx')
- grad_dual: float32 [3, 32, 256, 512], P(None, 'gz', 'gy', 'gx')
- sym_dual: float32 [6, 32, 256, 512], P(None, 'gz', 'gy', 'gx')
All inputs are finite; a program needn't handle non-finite values.
Results may differ from a plain program's by a relative error of at most 0.0001.
Values sent between devices are 32-bit elements; how exact they have to be, the bound alone decides.
A program may use at most 64 MiB of HBM per device.

v0:
```python
import jax
import jax.numpy as jnp
from jax import lax
from jax.sharding import PartitionSpec as P

ITERS = 3


first_alpha = 0.5
second_alpha = 1.0
dual_step = 0.2
primal_step = 0.2
index_pairs = ((0, 0), (1, 1), (2, 2), (0, 1), (0, 2), (1, 2))


def passed_along(shard, axis, by):
    devices = lax.axis_size(axis)
    pairs = [(i, i + by) for i in range(devices) if 0 <= i + by < devices]
    return lax.ppermute(shard, axis, pairs)


def pair_index(left_axis, right_axis):
    for position, entry_pair in enumerate(index_pairs):
        if entry_pair == (left_axis, right_axis) or entry_pair == (right_axis, left_axis):
            return position
    return 0


def first_layer(values, axis_dim):
    return lax.slice_in_dim(values, 0, 1, axis=axis_dim)


def last_layer(values, axis_dim):
    extent = values.shape[axis_dim]
    return lax.slice_in_dim(values, extent - 1, extent, axis=axis_dim)


def following(values, border, axis_dim):
    extent = values.shape[axis_dim]
    return jnp.concatenate(
        [lax.slice_in_dim(values, 1, extent, axis=axis_dim), border], axis=axis_dim
    )


def preceding(values, border, axis_dim):
    extent = values.shape[axis_dim]
    return jnp.concatenate(
        [border, lax.slice_in_dim(values, 0, extent - 1, axis=axis_dim)], axis=axis_dim
    )


def edge_masks(extents, margin):
    device_places = (lax.axis_index("gx"), lax.axis_index("gy"), lax.axis_index("gz"))
    group_sizes = (lax.axis_size("gx"), lax.axis_size("gy"), lax.axis_size("gz"))
    lower_masks = []
    upper_masks = []
    inside = jnp.ones((1, 1, 1, 1), jnp.float32)
    for component in range(3):
        extent = extents[2 - component]
        places = (
            device_places[component] * extent - margin + lax.iota(jnp.int32, extent + 2 * margin)
        )
        full_extent = group_sizes[component] * extent
        shape_list = [1, 1, 1, 1]
        shape_list[3 - component] = extent + 2 * margin
        upper_masks.append((places < full_extent - 1).astype(jnp.float32).reshape(shape_list))
        lower_masks.append((places > 0).astype(jnp.float32).reshape(shape_list))
        within = jnp.logical_and(places >= 0, places < full_extent)
        inside = inside * within.astype(jnp.float32).reshape(shape_list)
    return (lower_masks, upper_masks, inside)


def q_rows(stacked, column):
    return jnp.stack([stacked[pair_index(row_axis, column)] for row_axis in range(3)], axis=0)


def project(stacked, weights, bound):
    magnitude = jnp.sqrt(jnp.sum(weights * stacked * stacked, axis=0, keepdims=True))
    return stacked / jnp.maximum(1.0, magnitude / bound)


def dual_update(bar_u, bar_v, grad_dual, sym_dual, next_u, prev_v, lower_masks, upper_masks):
    grads = jnp.concatenate(
        [upper_masks[component] * (next_u[component] - bar_u) for component in range(3)], axis=0
    )
    trial_p = grad_dual + dual_step * (grads - bar_v)
    new_p = project(trial_p, jnp.ones((3, 1, 1, 1), jnp.float32), first_alpha)
    derivs = [lower_masks[component] * (bar_v - prev_v[component]) for component in range(3)]
    sym_parts = []
    for left_axis, right_axis in index_pairs:
        sym_parts.append(0.5 * (derivs[right_axis][left_axis] + derivs[left_axis][right_axis]))
    trial_q = sym_dual + dual_step * jnp.stack(sym_parts, axis=0)
    weights = jnp.array([1.0, 1.0, 1.0, 2.0, 2.0, 2.0], jnp.float32).reshape((6, 1, 1, 1))
    new_q = project(trial_q, weights, second_alpha)
    return (new_p, new_q)


def primal_update(
    image_u,
    vector_v,
    grad_dual,
    sym_dual,
    noisy,
    weight_map,
    prev_p,
    next_q,
    lower_masks,
    upper_masks,
):
    divergence = jnp.zeros_like(image_u)
    second_div = jnp.zeros_like(vector_v)
    for component in range(3):
        divergence = (
            divergence
            + upper_masks[component] * grad_dual[component : component + 1]
            - prev_p[component]
        )
        second_div = (
            second_div + next_q[component] - lower_masks[component] * q_rows(sym_dual, component)
        )
    new_u = (image_u + primal_step * divergence + primal_step * weight_map * noisy) / (
        1.0 + primal_step * weight_map
    )
    new_v = vector_v + primal_step * (grad_dual + second_div)
    return (new_u, new_v)


def per_device(noisy_image, fidelity, primal_u, primal_v, dual_p, dual_q):
    noisy = noisy_image[None]
    weight_map = fidelity[None]
    image_u = primal_u[None]
    vector_v = primal_v
    grad_dual = dual_p
    sym_dual = dual_q
    lower_masks, upper_masks, unused_inside = edge_masks(noisy_image.shape, 0)
    bar_u = image_u
    bar_v = vector_v
    for step_index in range(ITERS):
        next_u = [
            following(bar_u, passed_along(first_layer(bar_u, 3), "gx", -1), 3),
            following(bar_u, passed_along(first_layer(bar_u, 2), "gy", -1), 2),
            following(bar_u, passed_along(first_layer(bar_u, 1), "gz", -1), 1),
        ]
        prev_v = [
            preceding(bar_v, passed_along(last_layer(bar_v, 3), "gx", 1), 3),
            preceding(bar_v, passed_along(last_layer(bar_v, 2), "gy", 1), 2),
            preceding(bar_v, passed_along(last_layer(bar_v, 1), "gz", 1), 1),
        ]
        grad_dual, sym_dual = dual_update(
            bar_u, bar_v, grad_dual, sym_dual, next_u, prev_v, lower_masks, upper_masks
        )
        grad_x = grad_dual[0:1]
        grad_y = grad_dual[1:2]
        grad_z = grad_dual[2:3]
        prev_p = [
            preceding(grad_x, passed_along(last_layer(grad_x, 3), "gx", 1), 3),
            preceding(grad_y, passed_along(last_layer(grad_y, 2), "gy", 1), 2),
            preceding(grad_z, passed_along(last_layer(grad_z, 1), "gz", 1), 1),
        ]
        rows_x = q_rows(sym_dual, 0)
        rows_y = q_rows(sym_dual, 1)
        rows_z = q_rows(sym_dual, 2)
        next_q = [
            following(rows_x, passed_along(first_layer(rows_x, 3), "gx", -1), 3),
            following(rows_y, passed_along(first_layer(rows_y, 2), "gy", -1), 2),
            following(rows_z, passed_along(first_layer(rows_z, 1), "gz", -1), 1),
        ]
        new_u, new_v = primal_update(
            image_u,
            vector_v,
            grad_dual,
            sym_dual,
            noisy,
            weight_map,
            prev_p,
            next_q,
            lower_masks,
            upper_masks,
        )
        bar_u = 2.0 * new_u - image_u
        bar_v = 2.0 * new_v - vector_v
        image_u = new_u
        vector_v = new_v
    return (image_u[0], vector_v, grad_dual, sym_dual)


def solution(mesh):
    in_specs = (
        P("gz", "gy", "gx"),
        P("gz", "gy", "gx"),
        P("gz", "gy", "gx"),
        P(None, "gz", "gy", "gx"),
        P(None, "gz", "gy", "gx"),
        P(None, "gz", "gy", "gx"),
    )
    out_specs = (
        P("gz", "gy", "gx"),
        P(None, "gz", "gy", "gx"),
        P(None, "gz", "gy", "gx"),
        P(None, "gz", "gy", "gx"),
    )
    return jax.shard_map(
        per_device, mesh=mesh, in_specs=in_specs, out_specs=out_specs, check_vma=False
    )
```

profile of v0, /device:TPU:7, one launch (start us, length us, event | category | flops | bytes accessed | tf_op | source)
XLA Modules:
  0.0 196.7 jit_solution(4864874494500455913)
XLA Ops:
  1.5 2.4 %collective-permute-start.1 = (f32[1,8,1,128]{3,2,1,0:T(1,128)S(1)}, f32[1,8,1,128]{3,2,1,0:T(1,128)S(1)}, u32[]{:S(2)}, u32[]{:S(2)}) collective-permute-start(f32[1,8,1,128]{3,2,1,0:T(1,128)S(1)} %slice.594), channel_id=1, source_target_pairs={{4,0},{8,4},{12,8},{16,12},{20,16},{24,20},{28,24},{5,1},{9,5},{13... | collective-permute-start | bytes 12296 | tf_op jit(solution)/shard_map/ppermute | solution.py:19
  4.8 6.4 %collective-permute-start.10 = (f32[3,8,1,128]{3,1,2,0:T(8,128)S(1)}, f32[3,8,1,128]{3,1,2,0:T(8,128)S(1)}, u32[]{:S(2)}, u32[]{:S(2)}) collective-permute-start(f32[3,8,1,128]{3,1,2,0:T(8,128)S(1)} %bitcast.80), channel_id=1, source_target_pairs={{0,4},{4,8},{8,12},{12,16},{16,20},{20,24},{24,28},{1,5},{5,9},{9,... | collective-permute-start | bytes 36872 | tf_op jit(solution)/shard_map/ppermute | solution.py:19
  12.0 3.1 %collective-permute-start.2 = (f32[1,1,32,128]{3,2,1,0:T(8,128)S(1)}, f32[1,1,32,128]{3,2,1,0:T(8,128)S(1)}, u32[]{:S(2)}, u32[]{:S(2)}) collective-permute-start(f32[1,1,32,128]{3,2,1,0:T(8,128)S(1)} %slice.596), channel_id=1, source_target_pairs={{1,0},{2,1},{3,2},{5,4},{6,5},{7,6},{9,8},{10,9},{11,10},{13,12},{... | collective-permute-start | bytes 49160 | tf_op jit(solution)/shard_map/ppermute | solution.py:19
  16.0 3.4 %collective-permute-start.11 = (f32[3,1,32,128]{3,2,1,0:T(8,128)S(1)}, f32[3,1,32,128]{3,2,1,0:T(8,128)S(1)}, u32[]{:S(2)}, u32[]{:S(2)}) collective-permute-start(f32[3,1,32,128]{3,2,1,0:T(8,128)S(1)} %slice.489), channel_id=1, source_target_pairs={{0,1},{1,2},{2,3},{4,5},{5,6},{6,7},{8,9},{9,10},{10,11},{12,13},{... | collective-permute-start | bytes 147464 | tf_op jit(solution)/shard_map/ppermute | solution.py:19
  19.4 1.3 collective-permute-start
  21.9 4.1 %collective-permute-done = f32[1,8,32,1]{3,2,1,0:T(8,128)S(1)} collective-permute-done((f32[1,8,32,1]{3,2,1,0:T(8,128)S(1)}, f32[1,8,32,1]{3,2,1,0:T(8,128)S(1)}, u32[]{:S(2)}, u32[]{:S(2)}) %collective-permute-start) | collective-permute-done | bytes 1056 | tf_op jit(solution)/shard_map/ppermute | solution.py:19
  25.9 3.2 %collective-permute-start.9 = (f32[3,8,32,1]{3,2,1,0:T(8,128)S(1)}, f32[3,8,32,1]{3,2,1,0:T(8,128)S(1)}, u32[]{:S(2)}, u32[]{:S(2)}) collective-permute-start(f32[3,8,32,1]{3,2,1,0:T(8,128)S(1)} %slice.483), channel_id=1, source_target_pairs={{0,32},{32,64},{64,96},{1,33},{33,65},{65,97},{2,34},{34,66},{66,9... | collective-permute-start | bytes 9224 | tf_op jit(solution)/shard_map/ppermute | solution.py:19
  29.3 8.1 %collective-permute-done.9 = f32[3,8,32,1]{3,2,1,0:T(8,128)S(1)} collective-permute-done((f32[3,8,32,1]{3,2,1,0:T(8,128)S(1)}, f32[3,8,32,1]{3,2,1,0:T(8,128)S(1)}, u32[]{:S(2)}, u32[]{:S(2)}) %collective-permute-start.9) | collective-permute-done | bytes 3104 | tf_op jit(solution)/shard_map/ppermute | solution.py:19
  40.2 2.2 %collective-permute-start.4 = (f32[1,8,1,128]{3,2,1,0:T(1,128)S(1)}, f32[1,8,1,128]{3,2,1,0:T(1,128)S(1)}, u32[]{:S(2)}, u32[]{:S(2)}) collective-permute-start(f32[1,8,1,128]{3,2,1,0:T(1,128)S(1)} %slice.601), channel_id=1, source_target_pairs={{0,4},{4,8},{8,12},{12,16},{16,20},{20,24},{24,28},{1,5},{5,9},{9,... | collective-permute-start | bytes 12296 | tf_op jit(solution)/shard_map/ppermute | solution.py:19
  42.5 1.9 collective-permute-start.5
  44.4 4.1 %collective-permute-start.3 = (f32[1,8,32,1]{3,2,1,0:T(8,128)S(1)}, f32[1,8,32,1]{3,2,1,0:T(8,128)S(1)}, u32[]{:S(2)}, u32[]{:S(2)}) collective-permute-start(f32[1,8,32,1]{3,2,1,0:T(8,128)S(1)} %slice.598), channel_id=1, source_target_pairs={{0,32},{32,64},{64,96},{1,33},{33,65},{65,97},{2,34},{34,66},{66,9... | collective-permute-start | bytes 3080 | tf_op jit(solution)/shard_map/ppermute | solution.py:19
  48.7 2.2 %collective-permute-done.3 = f32[1,8,32,1]{3,2,1,0:T(8,128)S(1)} collective-permute-done((f32[1,8,32,1]{3,2,1,0:T(8,128)S(1)}, f32[1,8,32,1]{3,2,1,0:T(8,128)S(1)}, u32[]{:S(2)}, u32[]{:S(2)}) %collective-permute-start.3) | collective-permute-done | bytes 1056 | tf_op jit(solution)/shard_map/ppermute | solution.py:19
  51.1 2.9 %collective-permute-start.7 = (f32[1,8,1,128]{3,2,1,0:T(1,128)S(1)}, f32[1,8,1,128]{3,2,1,0:T(1,128)S(1)}, u32[]{:S(2)}, u32[]{:S(2)}) collective-permute-start(f32[1,8,1,128]{3,2,1,0:T(1,128)S(1)} %slice.609), channel_id=1, source_target_pairs={{4,0},{8,4},{12,8},{16,12},{20,16},{24,20},{28,24},{5,1},{9,5},{13... | collective-permute-start | bytes 12296 | tf_op jit(solution)/shard_map/ppermute | solution.py:19
  54.0 3.7 %collective-permute-start.8 = (f32[1,1,32,128]{3,2,1,0:T(8,128)S(1)}, f32[1,1,32,128]{3,2,1,0:T(8,128)S(1)}, u32[]{:S(2)}, u32[]{:S(2)}) collective-permute-start(f32[1,1,32,128]{3,2,1,0:T(8,128)S(1)} %slice.611), channel_id=1, source_target_pairs={{1,0},{2,1},{3,2},{5,4},{6,5},{7,6},{9,8},{10,9},{11,10},{13,12},{... | collective-permute-start | bytes 49160 | tf_op jit(solution)/shard_map/ppermute | solution.py:19
  57.7 1.3 collective-permute-start.6
  59.1 1.9 collective-permute-start.14
  61.0 1.9 collective-permute-start.13
  63.1 2.1 %collective-permute-done.6 = f32[1,8,32,1]{3,2,1,0:T(8,128)S(1)} collective-permute-done((f32[1,8,32,1]{3,2,1,0:T(8,128)S(1)}, f32[1,8,32,1]{3,2,1,0:T(8,128)S(1)}, u32[]{:S(2)}, u32[]{:S(2)}) %collective-permute-start.6) | collective-permute-done | bytes 1056 | tf_op jit(solution)/shard_map/ppermute | solution.py:19
  65.1 1.3 collective-permute-start.12
  66.6 11.4 %collective-permute-done.12 = f32[3,8,32,1]{3,2,1,0:T(8,128)S(1)} collective-permute-done((f32[3,8,32,1]{3,2,1,0:T(8,128)S(1)}, f32[3,8,32,1]{3,2,1,0:T(8,128)S(1)}, u32[]{:S(2)}, u32[]{:S(2)}) %collective-permute-start.12) | collective-permute-done | bytes 3104 | tf_op jit(solution)/shard_map/ppermute | solution.py:19
  78.7 5.9 %collective-permute-start.22 = (f32[3,8,1,128]{3,1,2,0:T(8,128)S(1)}, f32[3,8,1,128]{3,1,2,0:T(8,128)S(1)}, u32[]{:S(2)}, u32[]{:S(2)}) collective-permute-start(f32[3,8,1,128]{3,1,2,0:T(8,128)S(1)} %bitcast.83), channel_id=1, source_target_pairs={{0,4},{4,8},{8,12},{12,16},{16,20},{20,24},{24,28},{1,5},{5,9},{9,... | collective-permute-start | bytes 36872 | tf_op jit(solution)/shard_map/ppermute | solution.py:19
  84.6 3.1 %collective-permute-start.23 = (f32[3,1,32,128]{3,2,1,0:T(8,128)S(1)}, f32[3,1,32,128]{3,2,1,0:T(8,128)S(1)}, u32[]{:S(2)}, u32[]{:S(2)}) collective-permute-start(f32[3,1,32,128]{3,2,1,0:T(8,128)S(1)} %slice.659), channel_id=1, source_target_pairs={{0,1},{1,2},{2,3},{4,5},{5,6},{6,7},{8,9},{9,10},{10,11},{12,13},{... | collective-permute-start | bytes 147464 | tf_op jit(solution)/shard_map/ppermute | solution.py:19
  87.7 3.7 %collective-permute-start.21 = (f32[3,8,32,1]{3,2,1,0:T(8,128)S(1)}, f32[3,8,32,1]{3,2,1,0:T(8,128)S(1)}, u32[]{:S(2)}, u32[]{:S(2)}) collective-permute-start(f32[3,8,32,1]{3,2,1,0:T(8,128)S(1)} %slice.653), channel_id=1, source_target_pairs={{0,32},{32,64},{64,96},{1,33},{33,65},{65,97},{2,34},{34,66},{66,9... | collective-permute-start | bytes 9224 | tf_op jit(solution)/shard_map/ppermute | solution.py:19
  91.5 8.4 %collective-permute-done.21 = f32[3,8,32,1]{3,2,1,0:T(8,128)S(1)} collective-permute-done((f32[3,8,32,1]{3,2,1,0:T(8,128)S(1)}, f32[3,8,32,1]{3,2,1,0:T(8,128)S(1)}, u32[]{:S(2)}, u32[]{:S(2)}) %collective-permute-start.21) | collective-permute-done | bytes 3104 | tf_op jit(solution)/shard_map/ppermute | solution.py:19
  101.4 1.9 collective-permute-start.16
  103.3 1.9 collective-permute-start.17
  105.2 3.8 %collective-permute-start.15 = (f32[1,8,32,1]{3,2,1,0:T(8,128)S(1)}, f32[1,8,32,1]{3,2,1,0:T(8,128)S(1)}, u32[]{:S(2)}, u32[]{:S(2)}) collective-permute-start(f32[1,8,32,1]{3,2,1,0:T(8,128)S(1)} %slice.639), channel_id=1, source_target_pairs={{0,32},{32,64},{64,96},{1,33},{33,65},{65,97},{2,34},{34,66},{66,9... | collective-permute-start | bytes 3080 | tf_op jit(solution)/shard_map/ppermute | solution.py:19
  109.2 2.2 %collective-permute-done.15 = f32[1,8,32,1]{3,2,1,0:T(8,128)S(1)} collective-permute-done((f32[1,8,32,1]{3,2,1,0:T(8,128)S(1)}, f32[1,8,32,1]{3,2,1,0:T(8,128)S(1)}, u32[]{:S(2)}, u32[]{:S(2)}) %collective-permute-start.15) | collective-permute-done | bytes 1056 | tf_op jit(solution)/shard_map/ppermute | solution.py:19
  111.6 3.4 %collective-permute-start.19 = (f32[1,8,1,128]{3,2,1,0:T(1,128)S(1)}, f32[1,8,1,128]{3,2,1,0:T(1,128)S(1)}, u32[]{:S(2)}, u32[]{:S(2)}) collective-permute-start(f32[1,8,1,128]{3,2,1,0:T(1,128)S(1)} %slice.650), channel_id=1, source_target_pairs={{4,0},{8,4},{12,8},{16,12},{20,16},{24,20},{28,24},{5,1},{9,5},{13... | collective-permute-start | bytes 12296 | tf_op jit(solution)/shard_map/ppermute | solution.py:19
  115.0 3.5 %collective-permute-start.20 = (f32[1,1,32,128]{3,2,1,0:T(8,128)S(1)}, f32[1,1,32,128]{3,2,1,0:T(8,128)S(1)}, u32[]{:S(2)}, u32[]{:S(2)}) collective-permute-start(f32[1,1,32,128]{3,2,1,0:T(8,128)S(1)} %slice.652), channel_id=1, source_target_pairs={{1,0},{2,1},{3,2},{5,4},{6,5},{7,6},{9,8},{10,9},{11,10},{13,12},{... | collective-permute-start | bytes 49160 | tf_op jit(solution)/shard_map/ppermute | solution.py:19
  118.5 1.3 collective-permute-start.18
  119.9 1.9 collective-permute-start.26
  121.9 1.9 collective-permute-start.25
  123.9 2.1 %collective-permute-done.18 = f32[1,8,32,1]{3,2,1,0:T(8,128)S(1)} collective-permute-done((f32[1,8,32,1]{3,2,1,0:T(8,128)S(1)}, f32[1,8,32,1]{3,2,1,0:T(8,128)S(1)}, u32[]{:S(2)}, u32[]{:S(2)}) %collective-permute-start.18) | collective-permute-done | bytes 1056 | tf_op jit(solution)/shard_map/ppermute | solution.py:19
  127.4 11.4 %collective-permute-done.24 = f32[3,8,32,1]{3,2,1,0:T(8,128)S(1)} collective-permute-done((f32[3,8,32,1]{3,2,1,0:T(8,128)S(1)}, f32[3,8,32,1]{3,2,1,0:T(8,128)S(1)}, u32[]{:S(2)}, u32[]{:S(2)}) %collective-permute-start.24) | collective-permute-done | bytes 3104 | tf_op jit(solution)/shard_map/ppermute | solution.py:19
  139.5 6.4 %collective-permute-start.31 = (f32[3,8,1,128]{3,1,2,0:T(8,128)S(1)}, f32[3,8,1,128]{3,1,2,0:T(8,128)S(1)}, u32[]{:S(2)}, u32[]{:S(2)}) collective-permute-start(f32[3,8,1,128]{3,1,2,0:T(8,128)S(1)} %bitcast.84), channel_id=1, source_target_pairs={{0,4},{4,8},{8,12},{12,16},{16,20},{20,24},{24,28},{1,5},{5,9},{9,... | collective-permute-start | bytes 36872 | tf_op jit(solution)/shard_map/ppermute | solution.py:19
  146.0 2.8 %collective-permute-start.32 = (f32[3,1,32,128]{3,2,1,0:T(8,128)S(1)}, f32[3,1,32,128]{3,2,1,0:T(8,128)S(1)}, u32[]{:S(2)}, u32[]{:S(2)}) collective-permute-start(f32[3,1,32,128]{3,2,1,0:T(8,128)S(1)} %slice.700), channel_id=1, source_target_pairs={{0,1},{1,2},{2,3},{4,5},{5,6},{6,7},{8,9},{9,10},{10,11},{12,13},{... | collective-permute-start | bytes 147464 | tf_op jit(solution)/shard_map/ppermute | solution.py:19
  148.7 3.7 %collective-permute-start.30 = (f32[3,8,32,1]{3,2,1,0:T(8,128)S(1)}, f32[3,8,32,1]{3,2,1,0:T(8,128)S(1)}, u32[]{:S(2)}, u32[]{:S(2)}) collective-permute-start(f32[3,8,32,1]{3,2,1,0:T(8,128)S(1)} %slice.694), channel_id=1, source_target_pairs={{0,32},{32,64},{64,96},{1,33},{33,65},{65,97},{2,34},{34,66},{66,9... | collective-permute-start | bytes 9224 | tf_op jit(solution)/shard_map/ppermute | solution.py:19
  152.5 8.3 %collective-permute-done.30 = f32[3,8,32,1]{3,2,1,0:T(8,128)S(1)} collective-permute-done((f32[3,8,32,1]{3,2,1,0:T(8,128)S(1)}, f32[3,8,32,1]{3,2,1,0:T(8,128)S(1)}, u32[]{:S(2)}, u32[]{:S(2)}) %collective-permute-start.30) | collective-permute-done | bytes 3104 | tf_op jit(solution)/shard_map/ppermute | solution.py:19
  162.8 1.9 collective-permute-start.35
  164.8 1.9 collective-permute-start.34
  166.7 1.3 collective-permute-start.33
  168.1 11.5 %collective-permute-done.33 = f32[3,8,32,1]{3,2,1,0:T(8,128)S(1)} collective-permute-done((f32[3,8,32,1]{3,2,1,0:T(8,128)S(1)}, f32[3,8,32,1]{3,2,1,0:T(8,128)S(1)}, u32[]{:S(2)}, u32[]{:S(2)}) %collective-permute-start.33) | collective-permute-done | bytes 3104 | tf_op jit(solution)/shard_map/ppermute | solution.py:19
  179.6 1.3 fusion.13
  180.9 1.9 collective-permute-start.29
  182.9 7.4 %collective-permute-start.28 = (f32[1,8,1,128]{3,2,1,0:T(1,128)S(1)}, f32[1,8,1,128]{3,2,1,0:T(1,128)S(1)}, u32[]{:S(2)}, u32[]{:S(2)}) collective-permute-start(f32[1,8,1,128]{3,2,1,0:T(1,128)S(1)} %slice.689), channel_id=1, source_target_pairs={{0,4},{4,8},{8,12},{12,16},{16,20},{20,24},{24,28},{1,5},{5,9},{9,... | collective-permute-start | bytes 12296 | tf_op jit(solution)/shard_map/ppermute | solution.py:19
  190.3 3.6 %collective-permute-start.27 = (f32[1,8,32,1]{3,2,1,0:T(8,128)S(1)}, f32[1,8,32,1]{3,2,1,0:T(8,128)S(1)}, u32[]{:S(2)}, u32[]{:S(2)}) collective-permute-start(f32[1,8,32,1]{3,2,1,0:T(8,128)S(1)} %slice.686), channel_id=1, source_target_pairs={{0,32},{32,64},{64,96},{1,33},{33,65},{65,97},{2,34},{34,66},{66,9... | collective-permute-start | bytes 3080 | tf_op jit(solution)/shard_map/ppermute | solution.py:19
  194.0 1.9 collective-permute-done.27
  (163 shorter events, 15.4 us)
Async XLA Ops:
  0.6 18.8 %copy-start.3 = (f32[8,32,128]{2,1,0:T(8,128)S(1)}, f32[8,32,128]{2,1,0:T(8,128)}, u32[]{:S(2)}) copy-start(f32[8,32,128]{2,1,0:T(8,128)} %param.11) | copy-start | bytes 393220
  1.5 27.7 %collective-permute-start.1 = (f32[1,8,1,128]{3,2,1,0:T(1,128)S(1)}, f32[1,8,1,128]{3,2,1,0:T(1,128)S(1)}, u32[]{:S(2)}, u32[]{:S(2)}) collective-permute-start(f32[1,8,1,128]{3,2,1,0:T(1,128)S(1)} %slice.594), channel_id=1, source_target_pairs={{4,0},{8,4},{12,8},{16,12},{20,16},{24,20},{28,24},{5,1},{9,5},{13... | collective-permute-start | bytes 12296 | tf_op jit(solution)/shard_map/ppermute | solution.py:19
  4.8 32.7 %collective-permute-start.10 = (f32[3,8,1,128]{3,1,2,0:T(8,128)S(1)}, f32[3,8,1,128]{3,1,2,0:T(8,128)S(1)}, u32[]{:S(2)}, u32[]{:S(2)}) collective-permute-start(f32[3,8,1,128]{3,1,2,0:T(8,128)S(1)} %bitcast.80), channel_id=1, source_target_pairs={{0,4},{4,8},{8,12},{12,16},{16,20},{20,24},{24,28},{1,5},{5,9},{9,... | collective-permute-start | bytes 36872 | tf_op jit(solution)/shard_map/ppermute | solution.py:19
  12.0 17.2 %collective-permute-start.2 = (f32[1,1,32,128]{3,2,1,0:T(8,128)S(1)}, f32[1,1,32,128]{3,2,1,0:T(8,128)S(1)}, u32[]{:S(2)}, u32[]{:S(2)}) collective-permute-start(f32[1,1,32,128]{3,2,1,0:T(8,128)S(1)} %slice.596), channel_id=1, source_target_pairs={{1,0},{2,1},{3,2},{5,4},{6,5},{7,6},{9,8},{10,9},{11,10},{13,12},{... | collective-permute-start | bytes 49160 | tf_op jit(solution)/shard_map/ppermute | solution.py:19
  16.0 21.5 %collective-permute-start.11 = (f32[3,1,32,128]{3,2,1,0:T(8,128)S(1)}, f32[3,1,32,128]{3,2,1,0:T(8,128)S(1)}, u32[]{:S(2)}, u32[]{:S(2)}) collective-permute-start(f32[3,1,32,128]{3,2,1,0:T(8,128)S(1)} %slice.489), channel_id=1, source_target_pairs={{0,1},{1,2},{2,3},{4,5},{5,6},{6,7},{8,9},{9,10},{10,11},{12,13},{... | collective-permute-start | bytes 147464 | tf_op jit(solution)/shard_map/ppermute | solution.py:19
  19.4 6.5 %collective-permute-start = (f32[1,8,32,1]{3,2,1,0:T(8,128)S(1)}, f32[1,8,32,1]{3,2,1,0:T(8,128)S(1)}, u32[]{:S(2)}, u32[]{:S(2)}) collective-permute-start(f32[1,8,32,1]{3,2,1,0:T(8,128)S(1)} %bitcast.68), channel_id=1, source_target_pairs={{32,0},{64,32},{96,64},{33,1},{65,33},{97,65},{34,2},{66,34},{98,6... | collective-permute-start | bytes 3080 | tf_op jit(solution)/shard_map/ppermute | solution.py:19
  20.7 1.0 copy-start
  25.9 11.5 %collective-permute-start.9 = (f32[3,8,32,1]{3,2,1,0:T(8,128)S(1)}, f32[3,8,32,1]{3,2,1,0:T(8,128)S(1)}, u32[]{:S(2)}, u32[]{:S(2)}) collective-permute-start(f32[3,8,32,1]{3,2,1,0:T(8,128)S(1)} %slice.483), channel_id=1, source_target_pairs={{0,32},{32,64},{64,96},{1,33},{33,65},{65,97},{2,34},{34,66},{66,9... | collective-permute-start | bytes 9224 | tf_op jit(solution)/shard_map/ppermute | solution.py:19
  29.2 8.3 %copy-start.5 = (f32[3,8,32,128]{3,2,1,0:T(8,128)S(1)}, f32[3,8,32,128]{3,2,1,0:T(8,128)}, u32[]{:S(2)}) copy-start(f32[3,8,32,128]{3,2,1,0:T(8,128)} %param.13) | copy-start | bytes 1179652
  38.3 1.1 copy-start.4
  38.4 1.0 copy-start.8
  40.2 10.6 %collective-permute-start.4 = (f32[1,8,1,128]{3,2,1,0:T(1,128)S(1)}, f32[1,8,1,128]{3,2,1,0:T(1,128)S(1)}, u32[]{:S(2)}, u32[]{:S(2)}) collective-permute-start(f32[1,8,1,128]{3,2,1,0:T(1,128)S(1)} %slice.601), channel_id=1, source_target_pairs={{0,4},{4,8},{8,12},{12,16},{16,20},{20,24},{24,28},{1,5},{5,9},{9,... | collective-permute-start | bytes 12296 | tf_op jit(solution)/shard_map/ppermute | solution.py:19
  42.5 8.4 %collective-permute-start.5 = (f32[1,1,32,128]{3,2,1,0:T(8,128)S(1)}, f32[1,1,32,128]{3,2,1,0:T(8,128)S(1)}, u32[]{:S(2)}, u32[]{:S(2)}) collective-permute-start(f32[1,1,32,128]{3,2,1,0:T(8,128)S(1)} %slice.604), channel_id=1, source_target_pairs={{0,1},{1,2},{2,3},{4,5},{5,6},{6,7},{8,9},{9,10},{10,11},{12,13},{... | collective-permute-start | bytes 49160 | tf_op jit(solution)/shard_map/ppermute | solution.py:19
  44.4 6.5 %collective-permute-start.3 = (f32[1,8,32,1]{3,2,1,0:T(8,128)S(1)}, f32[1,8,32,1]{3,2,1,0:T(8,128)S(1)}, u32[]{:S(2)}, u32[]{:S(2)}) collective-permute-start(f32[1,8,32,1]{3,2,1,0:T(8,128)S(1)} %slice.598), channel_id=1, source_target_pairs={{0,32},{32,64},{64,96},{1,33},{33,65},{65,97},{2,34},{34,66},{66,9... | collective-permute-start | bytes 3080 | tf_op jit(solution)/shard_map/ppermute | solution.py:19
  48.6 2.2 %copy-start.6 = (f32[8,32,128]{2,1,0:T(8,128)S(1)}, f32[8,32,128]{2,1,0:T(8,128)}, u32[]{:S(2)}) copy-start(f32[8,32,128]{2,1,0:T(8,128)} %param.9) | copy-start | bytes 393220
  48.6 2.2 %copy-start.7 = (f32[8,32,128]{2,1,0:T(8,128)S(1)}, f32[8,32,128]{2,1,0:T(8,128)}, u32[]{:S(2)}) copy-start(f32[8,32,128]{2,1,0:T(8,128)} %param.10) | copy-start | bytes 393220
  51.1 15.3 %collective-permute-start.7 = (f32[1,8,1,128]{3,2,1,0:T(1,128)S(1)}, f32[1,8,1,128]{3,2,1,0:T(1,128)S(1)}, u32[]{:S(2)}, u32[]{:S(2)}) collective-permute-start(f32[1,8,1,128]{3,2,1,0:T(1,128)S(1)} %slice.609), channel_id=1, source_target_pairs={{4,0},{8,4},{12,8},{16,12},{20,16},{24,20},{28,24},{5,1},{9,5},{13... | collective-permute-start | bytes 12296 | tf_op jit(solution)/shard_map/ppermute | solution.py:19
  54.0 12.4 %collective-permute-start.8 = (f32[1,1,32,128]{3,2,1,0:T(8,128)S(1)}, f32[1,1,32,128]{3,2,1,0:T(8,128)S(1)}, u32[]{:S(2)}, u32[]{:S(2)}) collective-permute-start(f32[1,1,32,128]{3,2,1,0:T(8,128)S(1)} %slice.611), channel_id=1, source_target_pairs={{1,0},{2,1},{3,2},{5,4},{6,5},{7,6},{9,8},{10,9},{11,10},{13,12},{... | collective-permute-start | bytes 49160 | tf_op jit(solution)/shard_map/ppermute | solution.py:19
  57.7 7.4 %collective-permute-start.6 = (f32[1,8,32,1]{3,2,1,0:T(8,128)S(1)}, f32[1,8,32,1]{3,2,1,0:T(8,128)S(1)}, u32[]{:S(2)}, u32[]{:S(2)}) collective-permute-start(f32[1,8,32,1]{3,2,1,0:T(8,128)S(1)} %bitcast.73), channel_id=1, source_target_pairs={{32,0},{64,32},{96,64},{33,1},{65,33},{97,65},{34,2},{66,34},{98,6... | collective-permute-start | bytes 3080 | tf_op jit(solution)/shard_map/ppermute | solution.py:19
  59.1 18.9 %collective-permute-start.14 = (f32[3,1,32,128]{3,2,1,0:T(8,128)S(1)}, f32[3,1,32,128]{3,2,1,0:T(8,128)S(1)}, u32[]{:S(2)}, u32[]{:S(2)}) collective-permute-start(f32[3,1,32,128]{3,2,1,0:T(8,128)S(1)} %fusion.135), channel_id=1, source_target_pairs={{1,0},{2,1},{3,2},{5,4},{6,5},{7,6},{9,8},{10,9},{11,10},{13,12},{... | collective-permute-start | bytes 147464 | tf_op jit(solution)/shard_map/ppermute | solution.py:19
  61.0 17.0 %collective-permute-start.13 = (f32[3,8,1,128]{3,1,2,0:T(8,128)S(1)}, f32[3,8,1,128]{3,1,2,0:T(8,128)S(1)}, u32[]{:S(2)}, u32[]{:S(2)}) collective-permute-start(f32[3,8,1,128]{3,1,2,0:T(8,128)S(1)} %bitcast.81), channel_id=1, source_target_pairs={{4,0},{8,4},{12,8},{16,12},{20,16},{24,20},{28,24},{5,1},{9,5},{13... | collective-permute-start | bytes 36872 | tf_op jit(solution)/shard_map/ppermute | solution.py:19
  65.1 12.9 %collective-permute-start.12 = (f32[3,8,32,1]{3,2,1,0:T(8,128)S(1)}, f32[3,8,32,1]{3,2,1,0:T(8,128)S(1)}, u32[]{:S(2)}, u32[]{:S(2)}) collective-permute-start(f32[3,8,32,1]{3,2,1,0:T(8,128)S(1)} %fusion.8), channel_id=1, source_target_pairs={{32,0},{64,32},{96,64},{33,1},{65,33},{97,65},{34,2},{66,34},{98,6... | collective-permute-start | bytes 9224 | tf_op jit(solution)/shard_map/ppermute | solution.py:19
  78.7 21.2 %collective-permute-start.22 = (f32[3,8,1,128]{3,1,2,0:T(8,128)S(1)}, f32[3,8,1,128]{3,1,2,0:T(8,128)S(1)}, u32[]{:S(2)}, u32[]{:S(2)}) collective-permute-start(f32[3,8,1,128]{3,1,2,0:T(8,128)S(1)} %bitcast.83), channel_id=1, source_target_pairs={{0,4},{4,8},{8,12},{12,16},{16,20},{20,24},{24,28},{1,5},{5,9},{9,... | collective-permute-start | bytes 36872 | tf_op jit(solution)/shard_map/ppermute | solution.py:19
  84.6 15.3 %collective-permute-start.23 = (f32[3,1,32,128]{3,2,1,0:T(8,128)S(1)}, f32[3,1,32,128]{3,2,1,0:T(8,128)S(1)}, u32[]{:S(2)}, u32[]{:S(2)}) collective-permute-start(f32[3,1,32,128]{3,2,1,0:T(8,128)S(1)} %slice.659), channel_id=1, source_target_pairs={{0,1},{1,2},{2,3},{4,5},{5,6},{6,7},{8,9},{9,10},{10,11},{12,13},{... | collective-permute-start | bytes 147464 | tf_op jit(solution)/shard_map/ppermute | solution.py:19
  87.7 12.2 %collective-permute-start.21 = (f32[3,8,32,1]{3,2,1,0:T(8,128)S(1)}, f32[3,8,32,1]{3,2,1,0:T(8,128)S(1)}, u32[]{:S(2)}, u32[]{:S(2)}) collective-permute-start(f32[3,8,32,1]{3,2,1,0:T(8,128)S(1)} %slice.653), channel_id=1, source_target_pairs={{0,32},{32,64},{64,96},{1,33},{33,65},{65,97},{2,34},{34,66},{66,9... | collective-permute-start | bytes 9224 | tf_op jit(solution)/shard_map/ppermute | solution.py:19
  101.4 10.0 %collective-permute-start.16 = (f32[1,8,1,128]{3,2,1,0:T(1,128)S(1)}, f32[1,8,1,128]{3,2,1,0:T(1,128)S(1)}, u32[]{:S(2)}, u32[]{:S(2)}) collective-permute-start(f32[1,8,1,128]{3,2,1,0:T(1,128)S(1)} %slice.642), channel_id=1, source_target_pairs={{0,4},{4,8},{8,12},{12,16},{16,20},{20,24},{24,28},{1,5},{5,9},{9,... | collective-permute-start | bytes 12296 | tf_op jit(solution)/shard_map/ppermute | solution.py:19
  103.3 8.1 %collective-permute-start.17 = (f32[1,1,32,128]{3,2,1,0:T(8,128)S(1)}, f32[1,1,32,128]{3,2,1,0:T(8,128)S(1)}, u32[]{:S(2)}, u32[]{:S(2)}) collective-permute-start(f32[1,1,32,128]{3,2,1,0:T(8,128)S(1)} %slice.645), channel_id=1, source_target_pairs={{0,1},{1,2},{2,3},{4,5},{5,6},{6,7},{8,9},{9,10},{10,11},{12,13},{... | collective-permute-start | bytes 49160 | tf_op jit(solution)/shard_map/ppermute | solution.py:19
  105.2 6.2 %collective-permute-start.15 = (f32[1,8,32,1]{3,2,1,0:T(8,128)S(1)}, f32[1,8,32,1]{3,2,1,0:T(8,128)S(1)}, u32[]{:S(2)}, u32[]{:S(2)}) collective-permute-start(f32[1,8,32,1]{3,2,1,0:T(8,128)S(1)} %slice.639), channel_id=1, source_target_pairs={{0,32},{32,64},{64,96},{1,33},{33,65},{65,97},{2,34},{34,66},{66,9... | collective-permute-start | bytes 3080 | tf_op jit(solution)/shard_map/ppermute | solution.py:19
  111.6 15.6 %collective-permute-start.19 = (f32[1,8,1,128]{3,2,1,0:T(1,128)S(1)}, f32[1,8,1,128]{3,2,1,0:T(1,128)S(1)}, u32[]{:S(2)}, u32[]{:S(2)}) collective-permute-start(f32[1,8,1,128]{3,2,1,0:T(1,128)S(1)} %slice.650), channel_id=1, source_target_pairs={{4,0},{8,4},{12,8},{16,12},{20,16},{24,20},{28,24},{5,1},{9,5},{13... | collective-permute-start | bytes 12296 | tf_op jit(solution)/shard_map/ppermute | solution.py:19
  115.0 12.3 %collective-permute-start.20 = (f32[1,1,32,128]{3,2,1,0:T(8,128)S(1)}, f32[1,1,32,128]{3,2,1,0:T(8,128)S(1)}, u32[]{:S(2)}, u32[]{:S(2)}) collective-permute-start(f32[1,1,32,128]{3,2,1,0:T(8,128)S(1)} %slice.652), channel_id=1, source_target_pairs={{1,0},{2,1},{3,2},{5,4},{6,5},{7,6},{9,8},{10,9},{11,10},{13,12},{... | collective-permute-start | bytes 49160 | tf_op jit(solution)/shard_map/ppermute | solution.py:19
  118.5 7.4 %collective-permute-start.18 = (f32[1,8,32,1]{3,2,1,0:T(8,128)S(1)}, f32[1,8,32,1]{3,2,1,0:T(8,128)S(1)}, u32[]{:S(2)}, u32[]{:S(2)}) collective-permute-start(f32[1,8,32,1]{3,2,1,0:T(8,128)S(1)} %bitcast.72), channel_id=1, source_target_pairs={{32,0},{64,32},{96,64},{33,1},{65,33},{97,65},{34,2},{66,34},{98,6... | collective-permute-start | bytes 3080 | tf_op jit(solution)/shard_map/ppermute | solution.py:19
  119.9 18.9 %collective-permute-start.26 = (f32[3,1,32,128]{3,2,1,0:T(8,128)S(1)}, f32[3,1,32,128]{3,2,1,0:T(8,128)S(1)}, u32[]{:S(2)}, u32[]{:S(2)}) collective-permute-start(f32[3,1,32,128]{3,2,1,0:T(8,128)S(1)} %fusion.134), channel_id=1, source_target_pairs={{1,0},{2,1},{3,2},{5,4},{6,5},{7,6},{9,8},{10,9},{11,10},{13,12},{... | collective-permute-start | bytes 147464 | tf_op jit(solution)/shard_map/ppermute | solution.py:19
  121.9 17.0 %collective-permute-start.25 = (f32[3,8,1,128]{3,1,2,0:T(8,128)S(1)}, f32[3,8,1,128]{3,1,2,0:T(8,128)S(1)}, u32[]{:S(2)}, u32[]{:S(2)}) collective-permute-start(f32[3,8,1,128]{3,1,2,0:T(8,128)S(1)} %bitcast.82), channel_id=1, source_target_pairs={{4,0},{8,4},{12,8},{16,12},{20,16},{24,20},{28,24},{5,1},{9,5},{13... | collective-permute-start | bytes 36872 | tf_op jit(solution)/shard_map/ppermute | solution.py:19
  126.0 12.9 %collective-permute-start.24 = (f32[3,8,32,1]{3,2,1,0:T(8,128)S(1)}, f32[3,8,32,1]{3,2,1,0:T(8,128)S(1)}, u32[]{:S(2)}, u32[]{:S(2)}) collective-permute-start(f32[3,8,32,1]{3,2,1,0:T(8,128)S(1)} %fusion.6), channel_id=1, source_target_pairs={{32,0},{64,32},{96,64},{33,1},{65,33},{97,65},{34,2},{66,34},{98,6... | collective-permute-start | bytes 9224 | tf_op jit(solution)/shard_map/ppermute | solution.py:19
  139.5 21.2 %collective-permute-start.31 = (f32[3,8,1,128]{3,1,2,0:T(8,128)S(1)}, f32[3,8,1,128]{3,1,2,0:T(8,128)S(1)}, u32[]{:S(2)}, u32[]{:S(2)}) collective-permute-start(f32[3,8,1,128]{3,1,2,0:T(8,128)S(1)} %bitcast.84), channel_id=1, source_target_pairs={{0,4},{4,8},{8,12},{12,16},{16,20},{20,24},{24,28},{1,5},{5,9},{9,... | collective-permute-start | bytes 36872 | tf_op jit(solution)/shard_map/ppermute | solution.py:19
  146.0 14.8 %collective-permute-start.32 = (f32[3,1,32,128]{3,2,1,0:T(8,128)S(1)}, f32[3,1,32,128]{3,2,1,0:T(8,128)S(1)}, u32[]{:S(2)}, u32[]{:S(2)}) collective-permute-start(f32[3,1,32,128]{3,2,1,0:T(8,128)S(1)} %slice.700), channel_id=1, source_target_pairs={{0,1},{1,2},{2,3},{4,5},{5,6},{6,7},{8,9},{9,10},{10,11},{12,13},{... | collective-permute-start | bytes 147464 | tf_op jit(solution)/shard_map/ppermute | solution.py:19
  148.7 12.0 %collective-permute-start.30 = (f32[3,8,32,1]{3,2,1,0:T(8,128)S(1)}, f32[3,8,32,1]{3,2,1,0:T(8,128)S(1)}, u32[]{:S(2)}, u32[]{:S(2)}) collective-permute-start(f32[3,8,32,1]{3,2,1,0:T(8,128)S(1)} %slice.694), channel_id=1, source_target_pairs={{0,32},{32,64},{64,96},{1,33},{33,65},{65,97},{2,34},{34,66},{66,9... | collective-permute-start | bytes 9224 | tf_op jit(solution)/shard_map/ppermute | solution.py:19
  161.7 0.9 copy-start.1
  162.8 16.8 %collective-permute-start.35 = (f32[3,1,32,128]{3,2,1,0:T(8,128)S(1)}, f32[3,1,32,128]{3,2,1,0:T(8,128)S(1)}, u32[]{:S(2)}, u32[]{:S(2)}) collective-permute-start(f32[3,1,32,128]{3,2,1,0:T(8,128)S(1)} %fusion.133), channel_id=1, source_target_pairs={{1,0},{2,1},{3,2},{5,4},{6,5},{7,6},{9,8},{10,9},{11,10},{13,12},{... | collective-permute-start | bytes 147464 | tf_op jit(solution)/shard_map/ppermute | solution.py:19
  164.8 14.8 %collective-permute-start.34 = (f32[3,8,1,128]{3,1,2,0:T(8,128)S(1)}, f32[3,8,1,128]{3,1,2,0:T(8,128)S(1)}, u32[]{:S(2)}, u32[]{:S(2)}) collective-permute-start(f32[3,8,1,128]{3,1,2,0:T(8,128)S(1)} %bitcast.85), channel_id=1, source_target_pairs={{4,0},{8,4},{12,8},{16,12},{20,16},{24,20},{28,24},{5,1},{9,5},{13... | collective-permute-start | bytes 36872 | tf_op jit(solution)/shard_map/ppermute | solution.py:19
  166.7 12.9 %collective-permute-start.33 = (f32[3,8,32,1]{3,2,1,0:T(8,128)S(1)}, f32[3,8,32,1]{3,2,1,0:T(8,128)S(1)}, u32[]{:S(2)}, u32[]{:S(2)}) collective-permute-start(f32[3,8,32,1]{3,2,1,0:T(8,128)S(1)} %fusion.4), channel_id=1, source_target_pairs={{32,0},{64,32},{96,64},{33,1},{65,33},{97,65},{34,2},{66,34},{98,6... | collective-permute-start | bytes 9224 | tf_op jit(solution)/shard_map/ppermute | solution.py:19
  180.9 14.9 %copy-start.2 = (f32[3,8,32,128]{3,2,1,0:T(8,128)}, f32[3,8,32,128]{3,2,1,0:T(8,128)S(1)}, u32[]{:S(2)}) copy-start(f32[3,8,32,128]{3,2,1,0:T(8,128)S(1)} %get-tuple-element.17) | copy-start | bytes 1179652
  180.9 14.9 %collective-permute-start.29 = (f32[1,1,32,128]{3,2,1,0:T(8,128)S(1)}, f32[1,1,32,128]{3,2,1,0:T(8,128)S(1)}, u32[]{:S(2)}, u32[]{:S(2)}) collective-permute-start(f32[1,1,32,128]{3,2,1,0:T(8,128)S(1)} %slice.692), channel_id=1, source_target_pairs={{0,1},{1,2},{2,3},{4,5},{5,6},{6,7},{8,9},{9,10},{10,11},{12,13},{... | collective-permute-start | bytes 49160 | tf_op jit(solution)/shard_map/ppermute | solution.py:19
  182.9 13.0 %collective-permute-start.28 = (f32[1,8,1,128]{3,2,1,0:T(1,128)S(1)}, f32[1,8,1,128]{3,2,1,0:T(1,128)S(1)}, u32[]{:S(2)}, u32[]{:S(2)}) collective-permute-start(f32[1,8,1,128]{3,2,1,0:T(1,128)S(1)} %slice.689), channel_id=1, source_target_pairs={{0,4},{4,8},{8,12},{12,16},{16,20},{20,24},{24,28},{1,5},{5,9},{9,... | collective-permute-start | bytes 12296 | tf_op jit(solution)/shard_map/ppermute | solution.py:19
  190.3 5.5 %collective-permute-start.27 = (f32[1,8,32,1]{3,2,1,0:T(8,128)S(1)}, f32[1,8,32,1]{3,2,1,0:T(8,128)S(1)}, u32[]{:S(2)}, u32[]{:S(2)}) collective-permute-start(f32[1,8,32,1]{3,2,1,0:T(8,128)S(1)} %slice.686), channel_id=1, source_target_pairs={{0,32},{32,64},{64,96},{1,33},{33,65},{65,97},{2,34},{34,66},{66,9... | collective-permute-start | bytes 3080 | tf_op jit(solution)/shard_map/ppermute | solution.py:19
where the time goes:
time: 200 us; the launch traced here: 197 us
  starting transfers between devices  106 us (53%)
  waiting for transfers between devices  73.7 us (37%)
  other arithmetic  7.78 us (4%)
  local copies, waits for them, and re-layouts  7.62 us (4%)
    ppermute x36, starting transfers between devices, passed_along(): return lax.ppermute(shard, axis, pairs)  106 us
    ppermute x36, waiting for transfers between devices, passed_along(): return lax.ppermute(shard, axis, pairs)  73.7 us
  transfers between devices with their start and end apart: 36, of which 12 were waited for; matrix products, arithmetic and copies ran while one was open for 2% of the time, Pallas kernels for 0%

commit v1 on v0

v1 whole, which is shorter than its diff:
```python
import functools

import jax
import jax.numpy as jnp
from jax import lax
from jax.experimental import pallas as pl
from jax.experimental.pallas import tpu as pltpu
from jax.sharding import PartitionSpec as P

ITERS = 3
SIGMA = 0.2
TAU = 0.2
ALPHA1 = 0.5
ALPHA0 = 1.0
NZ, NY, NX = 8, 32, 128
TILES = NY // 8
ROWS = NY + 16
PROWS = NY + 8
Q_OF = ((0, 3, 4), (3, 1, 5), (4, 5, 2))
F32 = jnp.float32

(ZUP, ZDN, YUP, YDN, XUP, XDN, XUP_YDN, XDN_YUP, XUP_ZDN, XDN_ZUP, YUP_ZDN, YDN_ZUP,
 PZ, QZ, PY, QY, PX_, QX_) = range(18)
MOVES = {
    ZUP: (0, 0, 1), ZDN: (0, 0, -1), YUP: (0, 1, 0), YDN: (0, -1, 0), XUP: (1, 0, 0), XDN: (-1, 0, 0),
    XUP_YDN: (1, -1, 0), XDN_YUP: (-1, 1, 0), XUP_ZDN: (1, 0, -1), XDN_ZUP: (-1, 0, 1),
    YUP_ZDN: (0, 1, -1), YDN_ZUP: (0, -1, 1),
    PZ: (0, 0, 1), QZ: (0, 0, -1), PY: (0, 1, 0), QY: (0, -1, 0), PX_: (1, 0, 0), QX_: (-1, 0, 0),
}
N_BAR = 12


def p_step(p, here, following, v):
    t = [p[a] + SIGMA * ((following[a] - here) - v[a]) for a in range(3)]
    size = t[0] * t[0] + t[1] * t[1] + t[2] * t[2]
    scale = jnp.minimum(1.0, ALPHA1 * lax.rsqrt(size))
    return [scale * t[a] for a in range(3)]


def q_step(q, v, before):
    d = [[v[a] - before[b][a] for a in range(3)] for b in range(3)]
    s = [q[a] + SIGMA * d[a][a] for a in range(3)]
    s.append(q[3] + (0.5 * SIGMA) * (d[1][0] + d[0][1]))
    s.append(q[4] + (0.5 * SIGMA) * (d[2][0] + d[0][2]))
    s.append(q[5] + (0.5 * SIGMA) * (d[2][1] + d[1][2]))
    size = (s[0] * s[0] + s[1] * s[1] + s[2] * s[2]) + 2.0 * (s[3] * s[3] + s[4] * s[4] + s[5] * s[5])
    scale = jnp.minimum(1.0, ALPHA0 * lax.rsqrt(size))
    return [scale * s[i] for i in range(6)]


def kernel(sizes, f_in, w_in, u_in, v_in, p_in, q_in, u_out, v_out, p_out, q_out,
           bar, barx, uv, p, px, q, qx, fa, wb,
           xlo, xhi, ylo, yhi, e_a, e_b,
           xh_lo, xh_hi, yh_lo, yh_hi, d_xmyp, d_xpym, d_xmzp, d_xpzm, d_ymzp, d_ypzm,
           pyk, qyk, pxk, qxk, ply, quy, plxk, quxk, plx, qux,
           in_sem, out_sem, send_sem, recv_sem):
    names = ("gx", "gy", "gz")
    at = [lax.axis_index(n) for n in names]
    up = [at[i] < sizes[i] - 1 for i in range(3)]
    down = [at[i] > 0 for i in range(3)]

    def exists(move):
        flag = None
        for i in range(3):
            if move[i]:
                one = up[i] if move[i] > 0 else down[i]
                flag = one if flag is None else jnp.logical_and(flag, one)
        return flag

    def device(move):
        return {names[i]: at[i] + move[i] for i in range(3) if move[i]}

    def opposite(move):
        return tuple(-m for m in move)

    loads = [
        pltpu.make_async_copy(u_in, bar.at[0, 0, 1 : NZ + 1, 8 : 8 + NY, :], in_sem.at[0]),
        pltpu.make_async_copy(v_in, bar.at[0, 1:4, 1 : NZ + 1, 8 : 8 + NY, :], in_sem.at[1]),
        pltpu.make_async_copy(p_in, p.at[:, 1 : NZ + 1, 8 : 8 + NY, :], in_sem.at[2]),
        pltpu.make_async_copy(q_in, q.at[:, 0:NZ, 0:NY, :], in_sem.at[3]),
        pltpu.make_async_copy(f_in, fa, in_sem.at[4]),
        pltpu.make_async_copy(w_in, wb, in_sem.at[5]),
    ]
    for c in loads:
        c.start()

    barrier = pltpu.get_barrier_semaphore()
    arrivals = jnp.int32(0)
    for m in range(N_BAR):
        move = MOVES[m]
        arrivals = arrivals + exists(move).astype(jnp.int32)

        @pl.when(exists(move))
        def _():
            pl.semaphore_signal(
                barrier, inc=1, device_id=device(move), device_id_type=pl.DeviceIdType.MESH
            )

    def ends(m, r):
        if m == ZUP:
            return bar.at[r, :, NZ, 8 : 8 + NY, :], bar.at[r, :, 0, 8 : 8 + NY, :]
        if m == ZDN:
            return bar.at[r, :, 1, 8 : 8 + NY, :], bar.at[r, :, NZ + 1, 8 : 8 + NY, :]
        if m == PZ:
            return p_in.at[:, NZ - 1, :, :], p.at[:, 0, 8 : 8 + NY, :]
        if m == QZ:
            return q_in.at[:, 0, :, :], q.at[:, NZ, 0:NY, :]
        if m in (PY, QY, PX_, QX_):
            return {PY: (pyk, ply), QY: (qyk, quy), PX_: (pxk, plxk), QX_: (qxk, quxk)}[m]
        src, dst = {
            YUP: (yhi, yh_lo), YDN: (ylo, yh_hi), XUP: (xhi, xh_lo), XDN: (xlo, xh_hi),
            XUP_YDN: (xhi, d_xmyp), XDN_YUP: (xlo, d_xpym),
            XUP_ZDN: (xhi, d_xmzp), XDN_ZUP: (xlo, d_xpzm),
            YUP_ZDN: (e_a, d_ymzp), YDN_ZUP: (e_b, d_ypzm),
        }[m]
        return src.at[r], dst.at[r]

    def message(m, r):
        src, dst = ends(m, r)
        return pltpu.make_async_remote_copy(
            src_ref=src, dst_ref=dst, send_sem=send_sem.at[r, m], recv_sem=recv_sem.at[r, m],
            device_id=device(MOVES[m]), device_id_type=pl.DeviceIdType.MESH,
        )

    def messages(r):
        return range(18) if r == 0 else range(N_BAR)

    def send(r):
        for m in messages(r):
            @pl.when(exists(MOVES[m]))
            def _():
                message(m, r).start()

    def receive(r):
        for m in messages(r):
            @pl.when(exists(opposite(MOVES[m])))
            def _():
                message(m, r).wait_recv()

    lane = lax.broadcasted_iota(jnp.int32, (8, 128), 1)
    sub = lax.broadcasted_iota(jnp.int32, (8, 128), 0)

    def lanes(x, by):
        by = by % 128
        return x if isinstance(by, int) and by == 0 else pltpu.roll(x, by, 1)

    def subs(x, by):
        return pltpu.roll(x, by % 8, 0)

    first = lane == 0
    last = lane == 127

    def flagged(cond, x, other):
        return jnp.where(cond, x, other)

    def pack_pair(z, t, values, low, high):
        for f, x in enumerate(values):
            s = f * 32 + z * 4 + t
            rolled = pltpu.roll(x, s, 1)
            low = jnp.where(lane == s, rolled, low)
            high = jnp.where(lane == lax.rem(s + 127, 128), rolled, high)
        return low, high

    zero = jnp.zeros((8, 128), F32)

    def edges_out(r, z, t, values):
        for f, x in enumerate(values):
            if t == 0:
                ylo[r, f, pl.ds(z, 1), :] = x[0:1, :]
            if t == TILES - 1:
                yhi[r, f, pl.ds(z, 1), :] = x[7:8, :]

    def lines_out(r):
        for f in range(4):
            e_a[r, f : f + 1, :] = yhi[r, f, 0:1, :]
            e_b[r, f : f + 1, :] = ylo[r, f, NZ - 1 : NZ, :]

    def rolled_out(z, t, values):
        rows = pl.ds(8 * t, 8)
        barx[0, z, rows, :] = lanes(values[0], -1)
        for a in range(3):
            barx[1 + a, z, rows, :] = lanes(values[1 + a], 1)

    loads[0].wait()
    loads[1].wait()

    def first_pack(z, carry):
        low, high = carry
        for t in range(TILES):
            values = [bar[0, f, z + 1, 8 + 8 * t : 16 + 8 * t, :] for f in range(4)]
            low, high = pack_pair(z, t, values, low, high)
            edges_out(0, z, t, values)
            rolled_out(z, t, values)
        return low, high

    low, high = lax.fori_loop(0, NZ, first_pack, (zero, zero))
    xlo[0] = low
    xhi[0] = lanes(high, 1)
    lines_out(0)
    loads[2].wait()
    loads[3].wait()

    def pq_pack(z, carry):
        ph, q1, q2 = carry
        for t in range(TILES):
            for a in range(3):
                x = p[a, z + 1, 8 + 8 * t : 16 + 8 * t, :]
                s = a * 32 + z * 4 + t
                ph = jnp.where(lane == s, pltpu.roll(x, s + 1, 1), ph)
                if t == TILES - 1:
                    pyk[a, pl.ds(z, 1), :] = x[7:8, :]
            for i in range(6):
                x = q[i, z, 8 * t : 8 * t + 8, :]
                s = (i % 3) * 32 + z * 4 + t
                rolled = pltpu.roll(x, s, 1)
                if i < 3:
                    q1 = jnp.where(lane == s, rolled, q1)
                else:
                    q2 = jnp.where(lane == s, rolled, q2)
                if t == 0:
                    qyk[i, pl.ds(z, 1), :] = x[0:1, :]
        return ph, q1, q2

    ph, q1, q2 = lax.fori_loop(0, NZ, pq_pack, (zero, zero, zero))
    pxk[...] = ph
    qxk[0] = q1
    qxk[1] = q2

    pl.semaphore_wait(barrier, arrivals)
    send(0)

    loads[4].wait()
    loads[5].wait()

    def weights(z, carry):
        for t in range(TILES):
            rows = pl.ds(8 * t, 8)
            tw = TAU * wb[z, rows, :]
            fa[z, rows, :] = tw * fa[z, rows, :]
            wb[z, rows, :] = 1.0 / (1.0 + tw)
        return carry

    lax.fori_loop(0, NZ, weights, 0)

    def clamp(r):
        @pl.when(jnp.logical_not(up[0]))
        def _():
            xh_hi[r] = xhi[r]

        @pl.when(jnp.logical_not(down[0]))
        def _():
            xh_lo[r] = xlo[r]

        @pl.when(jnp.logical_not(up[1]))
        def _():
            yh_hi[r] = yhi[r]

        @pl.when(jnp.logical_not(down[1]))
        def _():
            yh_lo[r] = ylo[r]

        @pl.when(jnp.logical_not(up[2]))
        def _():
            bar[r, :, NZ + 1, 8 : 8 + NY, :] = bar[r, :, NZ, 8 : 8 + NY, :]

        @pl.when(jnp.logical_not(down[2]))
        def _():
            bar[r, :, 0, 8 : 8 + NY, :] = bar[r, :, 1, 8 : 8 + NY, :]

    mask_px = jnp.where(jnp.logical_and(last, jnp.logical_not(up[0])), 0.0, 1.0).astype(F32)
    mask_qx = jnp.where(jnp.logical_and(first, jnp.logical_not(down[0])), 0.0, 1.0).astype(F32)
    mask_py = jnp.where(jnp.logical_and(sub == 7, jnp.logical_not(up[1])), 0.0, 1.0).astype(F32)
    mask_qy = jnp.where(jnp.logical_and(sub == 0, jnp.logical_not(down[1])), 0.0, 1.0).astype(F32)

    in32 = lax.rem(lane, 32)
    in4 = lax.rem(lane, 4)

    def layers(r):
        low = xh_lo[r]
        a = subs(low, -1)
        edge = lanes(subs(d_xmyp[r], -1), 3)
        ny = jnp.where(sub < 7, a, jnp.where(in4 < 3, lanes(a, -1), flagged(up[1], edge, low)))
        nz = jnp.where(in32 < 28, lanes(low, -4), flagged(up[2], lanes(d_xmzp[r], 28), low))
        new = p_step([plx[c] for c in range(3)], low, [xlo[r], ny, nz],
                     [lanes(low, -32 * (1 + c)) for c in range(3)])
        for c in range(3):
            plx[c] = new[c]
        below_x = flagged(down[0], new[0], zero)

        high = xh_hi[r]
        a = subs(high, 1)
        edge = lanes(subs(d_xpym[r], 1), -3)
        py_ = jnp.where(sub > 0, a, jnp.where(in4 > 0, lanes(a, 1), flagged(down[1], edge, high)))
        pz_ = jnp.where(in32 >= 4, lanes(high, 4), flagged(down[2], lanes(d_xpzm[r], -28), high))
        own = xhi[r]

        def split(x):
            return [lanes(x, -32 * (1 + c)) for c in range(3)]

        new = q_step([qux[i] for i in range(6)], split(high), [split(own), split(py_), split(pz_)])
        for i in range(6):
            qux[i] = new[i]
        above_x = [flagged(up[0], new[i], zero) for i in Q_OF[0]]

        here = yh_lo[r, 0]
        row = jnp.broadcast_to(d_xpym[r, 7:8, :], (8, 128))
        col = jnp.sum(jnp.where(lane == 4 * sub + 3, row, 0.0), axis=1, keepdims=True)
        nx = jnp.where(lane < 127, lanes(here, -1), flagged(up[0], jnp.broadcast_to(col, (8, 128)), here))
        line = jnp.broadcast_to(d_ymzp[r, 0:1, :], (8, 128))
        nz = jnp.where(sub < 7, subs(here, -1), flagged(up[2], line, here))
        new = p_step([ply[c] for c in range(3)], here, [nx, ylo[r, 0], nz],
                     [yh_lo[r, 1 + c] for c in range(3)])
        for c in range(3):
            ply[c] = new[c]
        below_y = flagged(down[1], new[1], zero)
        for z in range(NZ):
            p[1, z + 1, 7:8, :] = below_y[z : z + 1, :]

        v = [yh_hi[r, 1 + c] for c in range(3)]
        row = jnp.broadcast_to(d_xmyp[r, 0:1, :], (8, 128))
        bx, bz = [], []
        for c in range(3):
            col = jnp.sum(jnp.where(lane == 4 * sub + 32 * (1 + c), row, 0.0), axis=1, keepdims=True)
            bx.append(jnp.where(lane > 0, lanes(v[c], 1),
                                flagged(down[0], jnp.broadcast_to(col, (8, 128)), v[c])))
            line = jnp.broadcast_to(d_ypzm[r, 1 + c : 2 + c, :], (8, 128))
            bz.append(jnp.where(sub > 0, subs(v[c], 1), flagged(down[2], line, v[c])))
        new = q_step([quy[i] for i in range(6)], v, [bx, [yhi[r, 1 + c] for c in range(3)], bz])
        for i in range(6):
            quy[i] = new[i]
        for i in Q_OF[1]:
            above_y = flagged(up[1], new[i], zero)
            for z in range(NZ):
                q[i, z, NY : NY + 1, :] = above_y[z : z + 1, :]

        bar[r, 0, 0, 8 + NY : 9 + NY, :] = flagged(up[1], d_ypzm[r, 0:1, :], bar[r, 0, 0, 7 + NY : 8 + NY, :])
        for c in range(3):
            bar[r, 1 + c, NZ + 1, 7:8, :] = flagged(down[1], d_ymzp[r, 1 + c : 2 + c, :],
                                                    bar[r, 1 + c, NZ + 1, 8:9, :])
        dn, du = d_xpzm[r], d_xmzp[r]
        for t in range(TILES):
            rows = slice(8 + 8 * t, 16 + 8 * t)
            here = bar[r, 0, 0, rows, :]
            nx = jnp.where(lane < 127, lanes(here, -1), flagged(up[0], lanes(dn, 127 - 28 - t), here))
            new = p_step([p[c, 0, rows, :] for c in range(3)], here,
                         [nx, bar[r, 0, 0, 9 + 8 * t : 17 + 8 * t, :], bar[r, 0, 1, rows, :]],
                         [bar[r, 1 + c, 0, rows, :] for c in range(3)])
            new[2] = flagged(down[2], new[2], zero)
            for c in range(3):
                p[c, 0, rows, :] = new[c]

            v = [bar[r, 1 + c, NZ + 1, rows, :] for c in range(3)]
            bx = [jnp.where(lane > 0, lanes(v[c], 1), flagged(down[0], lanes(du, -32 * (1 + c) - t), v[c]))
                  for c in range(3)]
            new = q_step([q[i, NZ, 8 * t : 8 * t + 8, :] for i in range(6)], v,
                         [bx, [bar[r, 1 + c, NZ + 1, 7 + 8 * t : 15 + 8 * t, :] for c in range(3)],
                          [bar[r, 1 + c, NZ, rows, :] for c in range(3)]])
            for i in range(6):
                value = flagged(up[2], new[i], zero) if i in Q_OF[2] else new[i]
                q[i, NZ, 8 * t : 8 * t + 8, :] = value
        return below_x, above_x

    def patch(r):
        high = xh_hi[r]
        low = xh_lo[r]
        for z in range(NZ):
            bar[r, 0, z + 1, 8 + NY : 9 + NY, :] = yh_hi[r, 0, z : z + 1, :]
            for c in range(3):
                bar[r, 1 + c, z + 1, 7:8, :] = yh_lo[r, 1 + c, z : z + 1, :]

        def body(z, carry):
            for t in range(TILES):
                rows = pl.ds(8 * t, 8)
                s = z * 4 + t
                old = barx[0, z, rows, :]
                barx[0, z, rows, :] = jnp.where(last, pltpu.roll(high, 127 - s, 1), old)
                for c in range(3):
                    old = barx[1 + c, z, rows, :]
                    barx[1 + c, z, rows, :] = jnp.where(
                        first, pltpu.roll(low, lax.rem(256 - 32 * (1 + c) - s, 128), 1), old)
            return carry

        lax.fori_loop(0, NZ, body, 0)

    def patch_pq(below_x, above_x):
        def body(z, carry):
            for t in range(TILES):
                rows = pl.ds(8 * t, 8)
                s = z * 4 + t
                px[z, rows, :] = jnp.where(first, pltpu.roll(below_x, lax.rem(128 - s, 128), 1), px[z, rows, :])
                for j in range(3):
                    qx[j, z, rows, :] = jnp.where(last, pltpu.roll(above_x[j], 127 - s, 1), qx[j, z, rows, :])
            return carry

        lax.fori_loop(0, NZ, body, 0)

    def dual(r):
        def body(z, carry):
            for t in range(TILES):
                rows = slice(8 + 8 * t, 16 + 8 * t)
                mine = slice(8 * t, 8 * t + 8)
                here = bar[r, 0, z + 1, rows, :]
                v = [bar[r, 1 + c, z + 1, rows, :] for c in range(3)]
                new = p_step([p[c, z + 1, rows, :] for c in range(3)], here,
                             [barx[0, z, mine, :], bar[r, 0, z + 1, 9 + 8 * t : 17 + 8 * t, :],
                              bar[r, 0, z + 2, rows, :]], v)
                for c in range(3):
                    p[c, z + 1, rows, :] = new[c]
                px[z, mine, :] = lanes(new[0], 1)
                new = q_step([q[i, z, mine, :] for i in range(6)], v,
                             [[barx[1 + c, z, mine, :] for c in range(3)],
                              [bar[r, 1 + c, z + 1, 7 + 8 * t : 15 + 8 * t, :] for c in range(3)],
                              [bar[r, 1 + c, z, rows, :] for c in range(3)]])
                for i in range(6):
                    q[i, z, mine, :] = new[i]
                for j, i in enumerate(Q_OF[0]):
                    qx[j, z, mine, :] = lanes(new[i], -1)
            return carry

        lax.fori_loop(0, NZ, body, 0)

    def primal(r):
        final = r == ITERS - 1

        def body(z, carry):
            low, high = carry
            mask_pz = jnp.where(jnp.logical_and(z == NZ - 1, jnp.logical_not(up[2])), 0.0, 1.0).astype(F32)
            mask_qz = jnp.where(jnp.logical_and(z == 0, jnp.logical_not(down[2])), 0.0, 1.0).astype(F32)
            for t in range(TILES):
                rows = slice(8 + 8 * t, 16 + 8 * t)
                mine = slice(8 * t, 8 * t + 8)
                pv = [p[c, z + 1, rows, :] for c in range(3)]
                div = mask_px * pv[0] - px[z, mine, :]
                own = mask_py * pv[1] if t == TILES - 1 else pv[1]
                div = div + own - p[1, z + 1, 7 + 8 * t : 15 + 8 * t, :]
                div = div + mask_pz * pv[2] - p[2, z, rows, :]
                if r == 0:
                    old = [bar[0, f, z + 1, rows, :] for f in range(4)]
                else:
                    old = [uv[f, z, mine, :] for f in range(4)]
                new = [(old[0] + TAU * div + fa[z, mine, :]) * wb[z, mine, :]]
                qv = [q[i, z, mine, :] for i in range(6)]
                for a in range(3):
                    ix, iy, iz = Q_OF[a]
                    total = qx[a, z, mine, :] - mask_qx * qv[ix]
                    own = mask_qy * qv[iy] if t == 0 else qv[iy]
                    total = total + q[iy, z, 1 + 8 * t : 9 + 8 * t, :] - own
                    total = total + q[iz, z + 1, mine, :] - mask_qz * qv[iz]
                    new.append(old[1 + a] + TAU * (pv[a] + total))
                for f in range(4):
                    uv[f, z, mine, :] = new[f]
                if not final:
                    values = [2.0 * new[f] - old[f] for f in range(4)]
                    for f in range(4):
                        bar[r + 1, f, z + 1, rows, :] = values[f]
                    low, high = pack_pair(z, t, values, low, high)
                    edges_out(r + 1, z, t, values)
                    rolled_out(z, t, values)
            return low, high

        low, high = lax.fori_loop(0, NZ, body, (zero, zero))
        if not final:
            xlo[r + 1] = low
            xhi[r + 1] = lanes(high, 1)
            lines_out(r + 1)

    stores = [
        pltpu.make_async_copy(p.at[:, 1 : NZ + 1, 8 : 8 + NY, :], p_out, out_sem.at[0]),
        pltpu.make_async_copy(q.at[:, 0:NZ, 0:NY, :], q_out, out_sem.at[1]),
        pltpu.make_async_copy(uv.at[0], u_out, out_sem.at[2]),
        pltpu.make_async_copy(uv.at[1:4], v_out, out_sem.at[3]),
    ]
    for r in range(ITERS):
        receive(r)
        clamp(r)
        if r == 0:
            packed = plxk[...]
            for c in range(3):
                plx[c] = lanes(packed, -32 * c)
            for i in range(6):
                qux[i] = lanes(quxk[i // 3], -32 * (i % 3))
        patch(r)
        below_x, above_x = layers(r)
        dual(r)
        patch_pq(below_x, above_x)
        if r == ITERS - 1:
            stores[0].start()
            stores[1].start()
        primal(r)
        if r < ITERS - 1:
            send(r + 1)
    stores[2].start()
    stores[3].start()
    for r in range(ITERS):
        for m in messages(r):
            @pl.when(exists(MOVES[m]))
            def _():
                message(m, r).wait_send()
    for c in stores:
        c.wait()


def per_device(sizes, *arrays):
    anywhere = pl.BlockSpec(memory_space=pl.ANY)
    tile = (8, 128)

    def vmem(*shape):
        return pltpu.VMEM(shape, F32)

    return pl.pallas_call(
        functools.partial(kernel, sizes),
        out_shape=tuple(jax.ShapeDtypeStruct(s, F32) for s in
                        ((NZ, NY, NX), (3, NZ, NY, NX), (3, NZ, NY, NX), (6, NZ, NY, NX))),
        in_specs=[anywhere] * 6,
        out_specs=(anywhere,) * 4,
        scratch_shapes=[
            vmem(ITERS, 4, NZ + 2, ROWS, NX),
            vmem(4, NZ, NY, NX),
            vmem(4, NZ, NY, NX),
            vmem(3, NZ + 1, PROWS, NX),
            vmem(NZ, NY, NX),
            vmem(6, NZ + 1, PROWS, NX),
            vmem(3, NZ, NY, NX),
            vmem(NZ, NY, NX),
            vmem(NZ, NY, NX),
            vmem(ITERS, *tile), vmem(ITERS, *tile),
            vmem(ITERS, 4, *tile), vmem(ITERS, 4, *tile),
            vmem(ITERS, 4, 128), vmem(ITERS, 4, 128),
            vmem(ITERS, *tile), vmem(ITERS, *tile),
            vmem(ITERS, 4, *tile), vmem(ITERS, 4, *tile),
            vmem(ITERS, *tile), vmem(ITERS, *tile), vmem(ITERS, *tile), vmem(ITERS, *tile),
            vmem(ITERS, 4, 128), vmem(ITERS, 4, 128),
            vmem(3, *tile), vmem(6, *tile), vmem(*tile), vmem(2, *tile),
            vmem(3, *tile), vmem(6, *tile), vmem(*tile), vmem(2, *tile),
            vmem(3, *tile), vmem(6, *tile),
            pltpu.SemaphoreType.DMA((6,)),
            pltpu.SemaphoreType.DMA((4,)),
            pltpu.SemaphoreType.DMA((ITERS, 18)),
            pltpu.SemaphoreType.DMA((ITERS, 18)),
        ],
        compiler_params=pltpu.CompilerParams(collective_id=0, has_side_effects=True),
        name="tgv",
    )(*arrays)


def solution(mesh):
    sizes = tuple(mesh.shape[n] for n in ("gx", "gy", "gz"))
    scalar = P("gz", "gy", "gx")
    stack = P(None, "gz", "gy", "gx")
    return jax.shard_map(
        functools.partial(per_device, sizes), mesh=mesh,
        in_specs=(scalar, scalar, scalar, stack, stack, stack),
        out_specs=(scalar, stack, stack, stack), check_vma=False,
    )
```

time: 200 us -> 37.5 us (0.19); the launches traced: 197 us -> 37.3 us
  starting transfers between devices: 106 us -> 0 us
  waiting for transfers between devices: 73.7 us -> 0 us
  Pallas kernels: 0 us -> 31.6 us
  other arithmetic: 7.78 us -> 0 us
  local copies, waits for them, and re-layouts: 7.62 us -> 5.09 us
    ppermute x36 -> x0, starting transfers between devices: 106 us -> none  [passed_along(): return lax.ppermute(shard, axis, pairs)]
    ppermute x36 -> x0, waiting for transfers between devices: 73.7 us -> none  [passed_along(): return lax.ppermute(shard, axis, pairs)]
    pallas_call x0 -> x1, Pallas kernels: none -> 31.6 us  [per_device(): pl.pallas_call(functools.partial(kernel, sizes), out_shape=tuple((jax.Sha...]
    slice x54 -> x0, local copies, waits for them, and re-layouts: 4.94 us -> none  [the longest x18 2.54 us: last_layer(): return lax.slice_in_dim(values, extent - 1, extent, axis=axis_dim)]
    unnamed x18 -> x8, local copies, waits for them, and re-layouts: 2.56 us -> 5.09 us
  transfers between devices with their start and end apart: 36 -> 0, of which waited for: 12 -> 0; matrix products, arithmetic and copies ran while one was open for 2% -> 0% of each run, Pallas kernels for 0% -> 0%
where the time goes in v1:
time: 37.5 us; the launch traced here: 37.3 us
  Pallas kernels  31.6 us (84%)
  local copies, waits for them, and re-layouts  5.09 us (14%)
  between operations  0.65 us (2%)
    pallas_call x1, Pallas kernels, per_device(): pl.pallas_call(functools.partial(kernel, sizes), out_shape=tuple((jax.Sha...  31.6 us
    unnamed x8, local copies, waits for them, and re-layouts  5.09 us

profile of v1, /device:TPU:7, one launch (start us, length us, event | category | flops | bytes accessed | tf_op | source)
XLA Modules:
  0.0 37.3 jit_solution(1491208753560278511)
XLA Ops:
  0.6 31.6 %tgv.1 = (f32[8,32,128]{2,1,0:T(8,128)}, f32[3,8,32,128]{3,2,1,0:T(8,128)}, f32[3,8,32,128]{3,2,1,0:T(8,128)}, f32[6,8,32,128]{3,2,1,0:T(8,128)}) custom-call(f32[8,32,128]{2,1,0:T(8,128)} %f_in.1, f32[8,32,128]{2,1,0:T(8,128)} %w_in.1, f32[8,32,128]{2,1,0:T(8,128)} %u_in.1, f32[3,8,32,128]{3,2,1,0:T(8,128)} %v_in.1, f32[3,8,32,128]{3,2,1,0:T(8,128)} %p_in.1, ...), custom_call_target="tpu_custom_call" | custom-call | tf_op jit(solution)/shard_map/tgv/pallas_call | solution.py:510
  32.2 0.0 copy-start.1
  32.2 1.6 %copy.14 = f32[8,32,128]{2,1,0:T(8,128)} copy(f32[8,32,128]{2,1,0:T(8,128)} %get-tuple-element.8) | data formatting | bytes 262144
  33.9 0.0 copy-start
  33.9 1.8 %copy.15 = f32[3,8,32,128]{3,2,1,0:T(8,128)} copy(f32[3,8,32,128]{3,2,1,0:T(8,128)} %get-tuple-element.9) | data formatting | bytes 786432
  35.7 0.0 copy-done.1
  35.7 0.7 %copy.16 = f32[3,8,32,128]{3,2,1,0:T(8,128)} copy(f32[3,8,32,128]{3,2,1,0:T(8,128)S(1)} %copy-done.1) | data formatting | bytes 786432
  36.5 0.0 copy-done
  36.5 0.9 %copy.17 = f32[6,8,32,128]{3,2,1,0:T(8,128)} copy(f32[6,8,32,128]{3,2,1,0:T(8,128)S(1)} %copy-done) | data formatting | bytes 1572864
Async XLA Ops:
  32.2 3.5 %copy-start.1 = (f32[3,8,32,128]{3,2,1,0:T(8,128)S(1)}, f32[3,8,32,128]{3,2,1,0:T(8,128)}, u32[]{:S(2)}) copy-start(f32[3,8,32,128]{3,2,1,0:T(8,128)} %get-tuple-element.10) | copy-start | bytes 1179652
  33.9 2.6 %copy-start = (f32[6,8,32,128]{3,2,1,0:T(8,128)S(1)}, f32[6,8,32,128]{3,2,1,0:T(8,128)}, u32[]{:S(2)}) copy-start(f32[6,8,32,128]{3,2,1,0:T(8,128)} %get-tuple-element.11) | copy-start | bytes 2359300

commit v2 on v1

v2 whole, which is shorter than its diff:
```python
import functools

import jax
import jax.numpy as jnp
from jax import lax
from jax.experimental import pallas as pl
from jax.experimental.pallas import tpu as pltpu
from jax.sharding import PartitionSpec as P

ITERS = 3
SIGMA = 0.2
TAU = 0.2
ALPHA1 = 0.5
ALPHA0 = 1.0
NZ, NY, NX = 8, 32, 128
TILES = NY // 8
ROWS = NY + 16
PROWS = NY + 8
Q_OF = ((0, 3, 4), (3, 1, 5), (4, 5, 2))
F32 = jnp.float32
NAMES = ("gx", "gy", "gz")

(ZUP, ZDN, YUP, YDN, XUP, XDN, XUP_YDN, XDN_YUP, XUP_ZDN, XDN_ZUP, YUP_ZDN, YDN_ZUP,
 PZ, QZ, PY, QY, PX_, QX_) = range(18)
MOVES = {
    ZUP: (0, 0, 1), ZDN: (0, 0, -1), YUP: (0, 1, 0), YDN: (0, -1, 0), XUP: (1, 0, 0), XDN: (-1, 0, 0),
    XUP_YDN: (1, -1, 0), XDN_YUP: (-1, 1, 0), XUP_ZDN: (1, 0, -1), XDN_ZUP: (-1, 0, 1),
    YUP_ZDN: (0, 1, -1), YDN_ZUP: (0, -1, 1),
    PZ: (0, 0, 1), QZ: (0, 0, -1), PY: (0, 1, 0), QY: (0, -1, 0), PX_: (1, 0, 0), QX_: (-1, 0, 0),
}
N_BAR = 12
FAR = (XUP_YDN, XDN_YUP, YUP, YDN, YUP_ZDN, YDN_ZUP)
NEAR = (ZDN, ZUP, XUP, XDN, XUP_ZDN, XDN_ZUP)
FAR0 = FAR + (QY, PY)
NEAR0 = NEAR + (QZ, PZ, PX_, QX_)
INNER = tuple(range(1, TILES - 1))
OUTER = (0, TILES - 1)
EVERY = tuple(range(TILES))


def p_step(p, here, following, v):
    t = [p[a] + SIGMA * ((following[a] - here) - v[a]) for a in range(3)]
    size = t[0] * t[0] + t[1] * t[1] + t[2] * t[2]
    scale = jnp.minimum(1.0, ALPHA1 * lax.rsqrt(size))
    return [scale * t[a] for a in range(3)]


def q_step(q, v, before):
    d = [[v[a] - before[b][a] for a in range(3)] for b in range(3)]
    s = [q[a] + SIGMA * d[a][a] for a in range(3)]
    s.append(q[3] + (0.5 * SIGMA) * (d[1][0] + d[0][1]))
    s.append(q[4] + (0.5 * SIGMA) * (d[2][0] + d[0][2]))
    s.append(q[5] + (0.5 * SIGMA) * (d[2][1] + d[1][2]))
    size = (s[0] * s[0] + s[1] * s[1] + s[2] * s[2]) + 2.0 * (s[3] * s[3] + s[4] * s[4] + s[5] * s[5])
    scale = jnp.minimum(1.0, ALPHA0 * lax.rsqrt(size))
    return [scale * s[i] for i in range(6)]


def lanes(x, by):
    return x if by % 128 == 0 else pltpu.roll(x, by % 128, 1)


def subs(x, by):
    return pltpu.roll(x, by % 8, 0)


def tile_iota(axis):
    return lax.broadcasted_iota(jnp.int32, (8, 128), axis)


def place(sizes):
    at = [lax.axis_index(n) for n in NAMES]
    return at, [at[i] < sizes[i] - 1 for i in range(3)], [at[i] > 0 for i in range(3)]


def primal_tile(z, t, masks, p, q, old, weight, below_x, above_x):
    first, last = masks[6], masks[7]
    rows = slice(8 + 8 * t, 16 + 8 * t)
    mine = slice(8 * t, 8 * t + 8)
    s = z * TILES + t
    pv = [p[c, z + 1, rows, :] for c in range(3)]
    div = masks[0] * pv[0] - jnp.where(first, lanes(below_x, -2 * s), lanes(pv[0], 1))
    div = div + ((masks[2] * pv[1] if t == TILES - 1 else pv[1]) - p[1, z + 1, 7 + 8 * t : 15 + 8 * t, :])
    div = div + ((masks[4] * pv[2] if z == NZ - 1 else pv[2]) - p[2, z, rows, :])
    fw, inverse = weight
    new = [(old[0] + TAU * div + fw) * inverse]
    bars = [2.0 * new[0] - old[0]]
    qv = [q[i, z, mine, :] for i in range(6)]
    qn = [jnp.where(last, lanes(above_x[j], 127 - 2 * s), lanes(qv[i], -1)) for j, i in enumerate(Q_OF[0])]
    for a in range(3):
        ix, iy, iz = Q_OF[a]
        total = pv[a] + (qn[a] - masks[1] * qv[ix])
        total = total + (q[iy, z, 1 + 8 * t : 9 + 8 * t, :] - (masks[3] * qv[iy] if t == 0 else qv[iy]))
        total = total + (q[iz, z + 1, mine, :] - (masks[5] * qv[iz] if z == 0 else qv[iz]))
        step = TAU * total
        new.append(old[1 + a] + step)
        bars.append(new[1 + a] + step)
    return new, bars


def edge_masks(up, down):
    lane, sub = tile_iota(1), tile_iota(0)
    first, last = lane == 0, lane == 127

    def at(where, inside):
        return jnp.where(jnp.logical_and(where, jnp.logical_not(inside)), 0.0, 1.0).astype(F32)

    return (at(last, up[0]), at(first, down[0]), at(sub == 7, up[1]), at(sub == 0, down[1]),
            jnp.where(up[2], 1.0, 0.0).astype(F32), jnp.where(down[2], 1.0, 0.0).astype(F32), first, last)


def exchange_kernel(sizes, f_in, w_in, u_in, v_in, p_in, q_in,
                    uv, p, q, fa, wb, cols,
                    bar0, bar1, bar2, xe, xey, xh_lo, xh_hi, d_xmyp, d_xpym, d_xmzp, d_xpzm,
                    pxk, qxk, plxk, quxk, plx, qux,
                    in_sem, send_sem, recv_sem):
    at, up, down = place(sizes)
    bars = (bar0, bar1, bar2)

    def exists(move):
        flag = None
        for i in range(3):
            if move[i]:
                one = up[i] if move[i] > 0 else down[i]
                flag = one if flag is None else jnp.logical_and(flag, one)
        return flag

    def device(move):
        return {NAMES[i]: at[i] + move[i] for i in range(3) if move[i]}

    def opposite(move):
        return tuple(-m for m in move)

    loads = [
        pltpu.make_async_copy(u_in, bar0.at[0, 1 : NZ + 1, 8 : 8 + NY, :], in_sem.at[0]),
        pltpu.make_async_copy(v_in, bar0.at[1:4, 1 : NZ + 1, 8 : 8 + NY, :], in_sem.at[1]),
        pltpu.make_async_copy(p_in, p.at[:, 1 : NZ + 1, 8 : 8 + NY, :], in_sem.at[2]),
        pltpu.make_async_copy(q_in, q.at[:, 0:NZ, 0:NY, :], in_sem.at[3]),
        pltpu.make_async_copy(f_in, fa, in_sem.at[4]),
        pltpu.make_async_copy(w_in, wb, in_sem.at[5]),
    ]
    barrier = pltpu.get_barrier_semaphore()
    arrivals = jnp.int32(0)
    for m in FAR + NEAR:
        move = MOVES[m]
        arrivals = arrivals + exists(move).astype(jnp.int32)

        @pl.when(exists(move))
        def _():
            pl.semaphore_signal(
                barrier, inc=1, device_id=device(move), device_id_type=pl.DeviceIdType.MESH
            )

    for c in loads:
        c.start()

    def ends(m, r):
        bar = bars[r]
        inner = slice(1, NZ + 1)
        if m == ZUP:
            return bar.at[:, NZ, 8 : 8 + NY, :], bar.at[:, 0, 8 : 8 + NY, :]
        if m == ZDN:
            return bar.at[:, 1, 8 : 8 + NY, :], bar.at[:, NZ + 1, 8 : 8 + NY, :]
        if m == YUP:
            return bar.at[:, 1 : NZ + 1, 7 + NY, :], bar.at[:, 1 : NZ + 1, 7, :]
        if m == YDN:
            return bar.at[:, 1 : NZ + 1, 8, :], bar.at[:, 1 : NZ + 1, 8 + NY, :]
        if m == YUP_ZDN:
            return bar.at[:, 1, 7 + NY, :], bar.at[:, NZ + 1, 7, :]
        if m == YDN_ZUP:
            return bar.at[:, NZ, 8, :], bar.at[:, 0, 8 + NY, :]
        if m == PZ:
            return p_in.at[:, NZ - 1, :, :], p.at[:, 0, 8 : 8 + NY, :]
        if m == QZ:
            return q_in.at[:, 0, :, :], q.at[:, NZ, 0:NY, :]
        if m == PY:
            return p_in.at[:, :, NY - 1, :], p.at[:, 1 : NZ + 1, 7, :]
        if m == QY:
            return q_in.at[:, :, 0, :], q.at[:, 0:NZ, NY, :]
        if m == PX_:
            return pxk, plxk
        if m == QX_:
            return qxk, quxk
        src, dst = {
            XUP: (xe, xh_lo), XDN: (xe, xh_hi), XUP_YDN: (xey, d_xmyp), XDN_YUP: (xey, d_xpym),
            XUP_ZDN: (xe, d_xmzp), XDN_ZUP: (xe, d_xpzm),
        }[m]
        return src.at[r], dst.at[r]

    def message(m, r):
        src, dst = ends(m, r)
        return pltpu.make_async_remote_copy(
            src_ref=src, dst_ref=dst, send_sem=send_sem.at[r, m], recv_sem=recv_sem.at[r, m],
            device_id=device(MOVES[m]), device_id_type=pl.DeviceIdType.MESH,
        )

    def send(r, which):
        for m in which:
            @pl.when(exists(MOVES[m]))
            def _():
                message(m, r).start()

    def receive(r, which):
        for m in which:
            @pl.when(exists(opposite(MOVES[m])))
            def _():
                message(m, r).wait_recv()

    lane, sub = tile_iota(1), tile_iota(0)
    first, last = lane == 0, lane == 127
    edge = jnp.logical_or(first, last)
    zero = jnp.zeros((8, 128), F32)
    masks = edge_masks(up, down)

    def pack_into(acc, z, t, values, mask, by):
        for f, x in enumerate(values):
            acc[f // 2] = acc[f // 2] + lanes(jnp.where(mask, x, 0.0), (f % 2) * 64 + 2 * (z * TILES + t) + by)

    loads[0].wait()
    loads[1].wait()
    acc = [zero, zero]
    for t in OUTER + INNER:
        for z in range(NZ):
            pack_into(acc, z, t, [bar0[f, z + 1, 8 + 8 * t : 16 + 8 * t, :] for f in range(4)], edge, 0)
        if t == OUTER[-1]:
            for h in range(2):
                xey[0, h] = acc[h]
    for h in range(2):
        xe[0, h] = acc[h]
    loads[2].wait()
    loads[3].wait()
    accp, accq = [zero, zero], [zero, zero, zero]
    for t in EVERY:
        for z in range(NZ):
            pack_into(accp, z, t, [p[a, z + 1, 8 + 8 * t : 16 + 8 * t, :] for a in range(3)], last, 1)
            pack_into(accq, z, t, [q[i, z, 8 * t : 8 * t + 8, :] for i in range(6)], first, 0)
    for h in range(2):
        pxk[h] = accp[h]
    for h in range(3):
        qxk[h] = accq[h]

    pl.semaphore_wait(barrier, arrivals)
    send(0, FAR0)
    send(0, NEAR0)

    loads[4].wait()
    loads[5].wait()
    for z in range(NZ):
        for t in EVERY:
            rows = slice(8 * t, 8 * t + 8)
            tw = TAU * wb[z, rows, :]
            fa[z, rows, :] = tw * fa[z, rows, :]
            wb[z, rows, :] = 1.0 / (1.0 + tw)

    def split(x):
        return [x[0], lanes(x[0], 64), x[1], lanes(x[1], 64)]

    def clamp_near(r):
        bar = bars[r]

        @pl.when(jnp.logical_not(up[0]))
        def _():
            for h in range(2):
                xh_hi[r, h] = lanes(xe[r, h], 1)

        @pl.when(jnp.logical_not(down[0]))
        def _():
            for h in range(2):
                xh_lo[r, h] = lanes(xe[r, h], -1)

        @pl.when(jnp.logical_not(up[2]))
        def _():
            bar[:, NZ + 1, 8 : 8 + NY, :] = bar[:, NZ, 8 : 8 + NY, :]

        @pl.when(jnp.logical_not(down[2]))
        def _():
            bar[:, 0, 8 : 8 + NY, :] = bar[:, 1, 8 : 8 + NY, :]

    def clamp_far(r):
        bar = bars[r]

        @pl.when(jnp.logical_not(up[2]))
        def _():
            for f in range(4):
                bar[f, NZ + 1, 7:8, :] = bar[f, NZ, 7:8, :]

        @pl.when(jnp.logical_not(down[2]))
        def _():
            for f in range(4):
                bar[f, 0, 8 + NY : 9 + NY, :] = bar[f, 1, 8 + NY : 9 + NY, :]

        @pl.when(jnp.logical_not(up[1]))
        def _():
            for f in range(4):
                bar[f, 0, 8 + NY : 9 + NY, :] = bar[f, 0, 7 + NY : 8 + NY, :]
                bar[f, 1 : NZ + 1, 8 + NY, :] = bar[f, 1 : NZ + 1, 7 + NY, :]

        @pl.when(jnp.logical_not(down[1]))
        def _():
            for f in range(4):
                bar[f, NZ + 1, 7:8, :] = bar[f, NZ + 1, 8:9, :]
                bar[f, 1 : NZ + 1, 7, :] = bar[f, 1 : NZ + 1, 8, :]

    in64 = lax.rem(lane, 64)
    in8 = lax.rem(lane, 8)

    def layers(r):
        bar = bars[r]
        own = [xe[r, h] for h in range(2)]
        own_high = [lanes(x, 1) for x in own]
        low = [lanes(xh_lo[r, h], 1) for h in range(2)]
        here = low[0]
        a = subs(here, -1)
        corner = lanes(subs(d_xmyp[r, 0], -1), 7)
        ny = jnp.where(sub < 7, a, jnp.where(in8 < 6, lanes(a, -2), jnp.where(up[1], corner, here)))
        nz = jnp.where(in64 < 56, lanes(here, -8), jnp.where(up[2], lanes(d_xmzp[r, 0], 57), here))
        new = p_step([plx[c] for c in range(3)], here, [own[0], ny, nz], split(low)[1:])
        for c in range(3):
            plx[c] = new[c]
        below_x = jnp.where(down[0], new[0], zero)

        high = [xh_hi[r, h] for h in range(2)]
        py_, pz_ = [], []
        for h in range(2):
            a = subs(high[h], 1)
            corner = lanes(subs(d_xpym[r, h], 1), -6)
            py_.append(jnp.where(sub > 0, a, jnp.where(in8 >= 2, lanes(a, 2), jnp.where(down[1], corner, high[h]))))
            pz_.append(jnp.where(in64 >= 8, lanes(high[h], 8),
                                 jnp.where(down[2], lanes(d_xpzm[r, h], -56), high[h])))
        new = q_step([qux[i] for i in range(6)], split(high)[1:],
                     [split(own_high)[1:], split(py_)[1:], split(pz_)[1:]])
        for i in range(6):
            qux[i] = new[i]
        above_x = [jnp.where(up[0], new[i], zero) for i in Q_OF[0]]

        inner, after, before = slice(1, NZ + 1), slice(2, NZ + 2), slice(0, NZ)
        here = bar[0, inner, 7, :]
        row = jnp.broadcast_to(d_xpym[r, 0, 7:8, :], (8, 128))
        col = jnp.sum(jnp.where(lane == 8 * sub + 6, row, 0.0), axis=1, keepdims=True)
        nx = jnp.where(lane < 127, lanes(here, -1), jnp.where(up[0], jnp.broadcast_to(col, (8, 128)), here))
        new = p_step([p[c, inner, 7, :] for c in range(3)], here,
                     [nx, bar[0, inner, 8, :], bar[0, after, 7, :]], [bar[1 + c, inner, 7, :] for c in range(3)])
        new[1] = jnp.where(down[1], new[1], zero)
        for c in range(3):
            p[c, inner, 7, :] = new[c]

        v = [bar[1 + c, inner, 8 + NY, :] for c in range(3)]
        bx = []
        for c in range(3):
            f = 1 + c
            row = jnp.broadcast_to(d_xmyp[r, f // 2, 0:1, :], (8, 128))
            source = lax.rem(8 * sub + (f % 2) * 64 + 127, 128)
            col = jnp.sum(jnp.where(lane == source, row, 0.0), axis=1, keepdims=True)
            bx.append(jnp.where(lane > 0, lanes(v[c], 1),
                                jnp.where(down[0], jnp.broadcast_to(col, (8, 128)), v[c])))
        new = q_step([q[i, before, NY, :] for i in range(6)], v,
                     [bx, [bar[1 + c, inner, 7 + NY, :] for c in range(3)],
                      [bar[1 + c, before, 8 + NY, :] for c in range(3)]])
        for i in range(6):
            q[i, before, NY, :] = jnp.where(up[1], new[i], zero) if i in Q_OF[1] else new[i]

        for t in EVERY:
            rows = slice(8 + 8 * t, 16 + 8 * t)
            here = bar[0, 0, rows, :]
            nx = jnp.where(lane < 127, lanes(here, -1),
                           jnp.where(up[0], lanes(d_xpzm[r, 0], 127 - 56 - 2 * t), here))
            new = p_step([p[c, 0, rows, :] for c in range(3)], here,
                         [nx, bar[0, 0, 9 + 8 * t : 17 + 8 * t, :], bar[0, 1, rows, :]],
                         [bar[1 + c, 0, rows, :] for c in range(3)])
            new[2] = jnp.where(down[2], new[2], zero)
            for c in range(3):
                p[c, 0, rows, :] = new[c]

            v = [bar[1 + c, NZ + 1, rows, :] for c in range(3)]
            bx = [jnp.where(lane > 0, lanes(v[c], 1),
                            jnp.where(down[0], lanes(d_xmzp[r, (1 + c) // 2], -((1 + c) % 2) * 64 - 2 * t + 1), v[c]))
                  for c in range(3)]
            new = q_step([q[i, NZ, 8 * t : 8 * t + 8, :] for i in range(6)], v,
                         [bx, [bar[1 + c, NZ + 1, 7 + 8 * t : 15 + 8 * t, :] for c in range(3)],
                          [bar[1 + c, NZ, rows, :] for c in range(3)]])
            for i in range(6):
                q[i, NZ, 8 * t : 8 * t + 8, :] = jnp.where(up[2], new[i], zero) if i in Q_OF[2] else new[i]
        return below_x, above_x

    def dual(r, tiles):
        bar = bars[r]
        high = xh_hi[r, 0]
        low = [xh_lo[r, h] for h in range(2)]
        for t in tiles:
            for z in range(NZ):
                rows = slice(8 + 8 * t, 16 + 8 * t)
                mine = slice(8 * t, 8 * t + 8)
                s = z * TILES + t
                here = bar[0, z + 1, rows, :]
                v = [bar[1 + c, z + 1, rows, :] for c in range(3)]
                nx = jnp.where(last, lanes(high, 127 - 2 * s), lanes(here, -1))
                new = p_step([p[c, z + 1, rows, :] for c in range(3)], here,
                             [nx, bar[0, z + 1, 9 + 8 * t : 17 + 8 * t, :], bar[0, z + 2, rows, :]], v)
                for c in range(3):
                    p[c, z + 1, rows, :] = new[c]
                bx = [jnp.where(first, lanes(low[(1 + c) // 2], 1 - ((1 + c) % 2) * 64 - 2 * s), lanes(v[c], 1))
                      for c in range(3)]
                new = q_step([q[i, z, mine, :] for i in range(6)], v,
                             [bx, [bar[1 + c, z + 1, 7 + 8 * t : 15 + 8 * t, :] for c in range(3)],
                              [bar[1 + c, z, rows, :] for c in range(3)]])
                for i in range(6):
                    q[i, z, mine, :] = new[i]

    def primal(r, tiles, acc, below_x, above_x):
        for t in tiles:
            for z in range(NZ):
                rows = slice(8 + 8 * t, 16 + 8 * t)
                mine = slice(8 * t, 8 * t + 8)
                if r == 0:
                    old = [bar0[f, z + 1, rows, :] for f in range(4)]
                else:
                    old = [uv[f, z, mine, :] for f in range(4)]
                new, values = primal_tile(z, t, masks, p, q, old, (fa[z, mine, :], wb[z, mine, :]), below_x, above_x)
                for f in range(4):
                    uv[f, z, mine, :] = new[f]
                    bars[r + 1][f, z + 1, rows, :] = values[f]
                pack_into(acc, z, t, values, edge, 0)

    for r in range(ITERS):
        receive(r, NEAR0 if r == 0 else NEAR)
        clamp_near(r)
        if r == 0:
            for c in range(3):
                plx[c] = lanes(plxk[c // 2], (c % 2) * 64)
            for i in range(6):
                qux[i] = lanes(quxk[i // 2], (i % 2) * 64)
        dual(r, INNER)
        receive(r, FAR0 if r == 0 else FAR)
        clamp_far(r)
        below_x, above_x = layers(r)
        dual(r, OUTER)
        if r < ITERS - 1:
            acc = [zero, zero]
            primal(r, OUTER, acc, below_x, above_x)
            for h in range(2):
                xey[r + 1, h] = acc[h]
            send(r + 1, FAR)
            primal(r, INNER, acc, below_x, above_x)
            for h in range(2):
                xe[r + 1, h] = acc[h]
            send(r + 1, NEAR)
    cols[0] = below_x
    for j in range(3):
        cols[1 + j] = above_x[j]
    for r in range(ITERS):
        for m in (FAR0 + NEAR0 if r == 0 else FAR + NEAR):
            @pl.when(exists(MOVES[m]))
            def _():
                message(m, r).wait_send()


def final_kernel(sizes, uv, p, q, fa, wb, cols, u_out, v_out, p_out, q_out, new_uv, out_sem):
    _, up, down = place(sizes)
    masks = edge_masks(up, down)
    stores = [
        pltpu.make_async_copy(p.at[:, 1 : NZ + 1, 8 : 8 + NY, :], p_out, out_sem.at[0]),
        pltpu.make_async_copy(q.at[:, 0:NZ, 0:NY, :], q_out, out_sem.at[1]),
    ]
    for c in stores:
        c.start()
    below_x = cols[0]
    above_x = [cols[1 + j] for j in range(3)]
    for z in range(NZ):
        for t in EVERY:
            mine = slice(8 * t, 8 * t + 8)
            new, _ = primal_tile(z, t, masks, p, q, [uv[f, z, mine, :] for f in range(4)],
                                 (fa[z, mine, :], wb[z, mine, :]), below_x, above_x)
            for f in range(4):
                new_uv[f, z, mine, :] = new[f]
        if z % 4 == 3:
            part = slice(z - 3, z + 1)
            more = [
                pltpu.make_async_copy(new_uv.at[0, part], u_out.at[part], out_sem.at[2 + z // 4]),
                pltpu.make_async_copy(new_uv.at[1:4, part], v_out.at[:, part], out_sem.at[4 + z // 4]),
            ]
            for c in more:
                c.start()
            stores += more
    for c in stores:
        c.wait()


def per_device(sizes, *arrays):
    hbm = pl.BlockSpec(memory_space=pltpu.HBM)
    here = pl.BlockSpec(memory_space=pltpu.VMEM)
    tile = (8, 128)

    def vmem(*shape):
        return pltpu.VMEM(shape, F32)

    state = pl.pallas_call(
        functools.partial(exchange_kernel, sizes),
        out_shape=(
            vmem(4, NZ, NY, NX),
            vmem(3, NZ + 1, PROWS, NX),
            vmem(6, NZ + 1, PROWS, NX),
            vmem(NZ, NY, NX),
            vmem(NZ, NY, NX),
            vmem(4, *tile),
        ),
        in_specs=[hbm] * 6,
        out_specs=(here,) * 6,
        scratch_shapes=[
            vmem(4, NZ + 2, ROWS, NX), vmem(4, NZ + 2, ROWS, NX), vmem(4, NZ + 2, ROWS, NX),
            vmem(ITERS, 2, *tile), vmem(ITERS, 2, *tile),
            vmem(ITERS, 2, *tile), vmem(ITERS, 2, *tile),
            vmem(ITERS, 2, *tile), vmem(ITERS, 2, *tile), vmem(ITERS, 2, *tile), vmem(ITERS, 2, *tile),
            vmem(2, *tile), vmem(3, *tile), vmem(2, *tile), vmem(3, *tile),
            vmem(3, *tile), vmem(6, *tile),
            pltpu.SemaphoreType.DMA((6,)),
            pltpu.SemaphoreType.DMA((ITERS, 18)),
            pltpu.SemaphoreType.DMA((ITERS, 18)),
        ],
        compiler_params=pltpu.CompilerParams(
            collective_id=0, has_side_effects=True, vmem_limit_bytes=24 << 20
        ),
        name="tgv_rounds",
    )(*[pltpu.with_memory_space_constraint(a, pltpu.HBM) for a in arrays])
    return pl.pallas_call(
        functools.partial(final_kernel, sizes),
        out_shape=tuple(jax.ShapeDtypeStruct(s, F32) for s in
                        ((NZ, NY, NX), (3, NZ, NY, NX), (3, NZ, NY, NX), (6, NZ, NY, NX))),
        in_specs=[here] * 6,
        out_specs=(hbm,) * 4,
        scratch_shapes=[vmem(4, NZ, NY, NX), pltpu.SemaphoreType.DMA((6,))],
        compiler_params=pltpu.CompilerParams(vmem_limit_bytes=24 << 20),
        name="tgv_last",
    )(*state)


def solution(mesh):
    sizes = tuple(mesh.shape[n] for n in NAMES)
    scalar = P("gz", "gy", "gx")
    stack = P(None, "gz", "gy", "gx")
    return jax.shard_map(
        functools.partial(per_device, sizes), mesh=mesh,
        in_specs=(scalar, scalar, scalar, stack, stack, stack),
        out_specs=(scalar, stack, stack, stack), check_vma=False,
    )
```

time: 37.5 us -> 25.2 us (0.67)
  Pallas kernels: 31.6 us -> 24.4 us
  local copies, waits for them, and re-layouts: 5.09 us -> 0 us
    pallas_call x1 -> x2, Pallas kernels: 31.6 us -> 24.4 us  [the longest x1 23.1 us: per_device(): pl.pallas_call(functools.partial(exchange_kernel, sizes), out_shape=(vmem...]
    unnamed x8 -> x0, local copies, waits for them, and re-layouts: 5.09 us -> none
where the time goes in v2:
time: 25.2 us; the launch traced here: 25 us
  Pallas kernels  24.4 us (97%)
  between operations  0.64 us (3%)
    pallas_call x1, Pallas kernels, per_device(): pl.pallas_call(functools.partial(exchange_kernel, sizes), out_shape=(vmem...  23.1 us
    pallas_call x1, Pallas kernels, per_device(): pl.pallas_call(functools.partial(final_kernel, sizes), out_shape=tuple((j...  1.23 us

profile of v2, /device:TPU:7, one launch (start us, length us, event | category | flops | bytes accessed | tf_op | source)
XLA Modules:
  0.0 25.0 jit_solution(3606328420143973236)
XLA Ops:
  0.6 23.1 %tgv_rounds.1 = (f32[4,8,32,128]{3,2,1,0:T(8,128)S(1)}, f32[3,9,40,128]{3,2,1,0:T(8,128)S(1)}, f32[6,9,40,128]{3,2,1,0:T(8,128)S(1)}, f32[8,32,128]{2,1,0:T(8,12...) custom-call(f32[8,32,128]{2,1,0:T(8,128)} %f_in.1, f32[8,32,128]{2,1,0:T(8,128)} %w_in.1, ...), custom_call_target="tpu_custom_call" | custom-call | tf_op jit(solution)/shard_map/tgv_rounds/pallas_call | solution.py:496
  23.8 1.2 %tgv_last.1 = (f32[8,32,128]{2,1,0:T(8,128)}, f32[3,8,32,128]{3,2,1,0:T(8,128)}, f32[3,8,32,128]{3,2,1,0:T(8,128)}, f32[6,8,32,128]{3,2,1,0:T(8,128)}) custom-call(f32[4,8,32,128]{3,2,1,0:T(8,128)S(1)} %get-tuple-element.10.uv, f32[3,9,40,128]{3,2,1,0:T(8,128)S(1)} %get-tuple-element.11.p, f32[6,9,40,128]{3,2,1,0:T(8,128)S(1)} %get-tuple-element.12.q, ...), custom_call_target="tpu_custom_call" | custom-call | tf_op jit(solution)/shard_map/tgv_last/pallas_call | solution.py:524

commit v3 on v2

--- a/solution.py
+++ b/solution.py
@@ -111,7 +111,7 @@
 
 def exchange_kernel(sizes, f_in, w_in, u_in, v_in, p_in, q_in,
                     uv, p, q, fa, wb, cols,
-                    bar0, bar1, bar2, xe, xey, xh_lo, xh_hi, d_xmyp, d_xpym, d_xmzp, d_xpzm,
+                    bar0, bar1, bar2, xe, kept, xh_lo, xh_hi, d_xmyp, d_xpym, d_xmzp, d_xpzm,
                     pxk, qxk, plxk, quxk, plx, qux,
                     in_sem, send_sem, recv_sem):
     at, up, down = place(sizes)
@@ -177,12 +177,16 @@
             return p_in.at[:, :, NY - 1, :], p.at[:, 1 : NZ + 1, 7, :]
         if m == QY:
             return q_in.at[:, :, 0, :], q.at[:, 0:NZ, NY, :]
+        if m == XUP_YDN:
+            return xe.at[r, :, 0, :], d_xmyp.at[r, :, 0, :]
+        if m == XDN_YUP:
+            return xe.at[r, :, 7, :], d_xpym.at[r, :, 7, :]
         if m == PX_:
             return pxk, plxk
         if m == QX_:
             return qxk, quxk
         src, dst = {
-            XUP: (xe, xh_lo), XDN: (xe, xh_hi), XUP_YDN: (xey, d_xmyp), XDN_YUP: (xey, d_xpym),
+            XUP: (xe, xh_lo), XDN: (xe, xh_hi),
             XUP_ZDN: (xe, d_xmzp), XDN_ZUP: (xe, d_xpzm),
         }[m]
         return src.at[r], dst.at[r]
@@ -222,9 +226,6 @@
     for t in OUTER + INNER:
         for z in range(NZ):
             pack_into(acc, z, t, [bar0[f, z + 1, 8 + 8 * t : 16 + 8 * t, :] for f in range(4)], edge, 0)
-        if t == OUTER[-1]:
-            for h in range(2):
-                xey[0, h] = acc[h]
     for h in range(2):
         xe[0, h] = acc[h]
     loads[2].wait()
@@ -304,40 +305,74 @@
     in64 = lax.rem(lane, 64)
     in8 = lax.rem(lane, 8)
 
-    def layers(r):
-        bar = bars[r]
+    def x_layers(r, corners):
         own = [xe[r, h] for h in range(2)]
         own_high = [lanes(x, 1) for x in own]
         low = [lanes(xh_lo[r, h], 1) for h in range(2)]
         here = low[0]
         a = subs(here, -1)
-        corner = lanes(subs(d_xmyp[r, 0], -1), 7)
-        ny = jnp.where(sub < 7, a, jnp.where(in8 < 6, lanes(a, -2), jnp.where(up[1], corner, here)))
+        corner = jnp.where(up[1], lanes(subs(d_xmyp[r, 0], -1), 7), here) if corners else here
+        ny = jnp.where(sub < 7, a, jnp.where(in8 < 6, lanes(a, -2), corner))
         nz = jnp.where(in64 < 56, lanes(here, -8), jnp.where(up[2], lanes(d_xmzp[r, 0], 57), here))
         new = p_step([plx[c] for c in range(3)], here, [own[0], ny, nz], split(low)[1:])
-        for c in range(3):
-            plx[c] = new[c]
+        if corners:
+            for c in range(3):
+                plx[c] = new[c]
         below_x = jnp.where(down[0], new[0], zero)
 
         high = [xh_hi[r, h] for h in range(2)]
         py_, pz_ = [], []
         for h in range(2):
             a = subs(high[h], 1)
-            corner = lanes(subs(d_xpym[r, h], 1), -6)
-            py_.append(jnp.where(sub > 0, a, jnp.where(in8 >= 2, lanes(a, 2), jnp.where(down[1], corner, high[h]))))
+            corner = jnp.where(down[1], lanes(subs(d_xpym[r, h], 1), -6), high[h]) if corners else high[h]
+            py_.append(jnp.where(sub > 0, a, jnp.where(in8 >= 2, lanes(a, 2), corner)))
             pz_.append(jnp.where(in64 >= 8, lanes(high[h], 8),
                                  jnp.where(down[2], lanes(d_xpzm[r, h], -56), high[h])))
         new = q_step([qux[i] for i in range(6)], split(high)[1:],
                      [split(own_high)[1:], split(py_)[1:], split(pz_)[1:]])
+        if corners:
+            for i in range(6):
+                qux[i] = new[i]
+        return below_x, [jnp.where(up[0], new[i], zero) for i in Q_OF[0]]
+
+    def high_column(source, f):
+        row = jnp.broadcast_to(source[f // 2, 0:1, :], (8, 128))
+        picked = jnp.where(lane == lax.rem(8 * sub + (f % 2) * 64 + 127, 128), row, 0.0)
+        return jnp.broadcast_to(jnp.sum(picked, axis=1, keepdims=True), (8, 128))
+
+    def low_column(source):
+        row = jnp.broadcast_to(source[0, 7:8, :], (8, 128))
+        return jnp.broadcast_to(jnp.sum(jnp.where(lane == 8 * sub + 6, row, 0.0), axis=1, keepdims=True), (8, 128))
+
+    inner, after, before = slice(1, NZ + 1), slice(2, NZ + 2), slice(0, NZ)
+
+    def keep_rows(r):
+        for c in range(3):
+            kept[c] = p[c, inner, 7 + NY, :]
+            kept[10 + c] = high_column(xh_lo.at[r], 1 + c)
         for i in range(6):
-            qux[i] = new[i]
-        above_x = [jnp.where(up[0], new[i], zero) for i in Q_OF[0]]
-
-        inner, after, before = slice(1, NZ + 1), slice(2, NZ + 2), slice(0, NZ)
+            kept[3 + i] = q[i, before, 0, :]
+        kept[9] = low_column(xh_hi.at[r])
+
+    def redo_rows(r):
+        bar = bars[r]
+        here = bar[0, inner, 7 + NY, :]
+        nx = jnp.where(last, kept[9], lanes(here, -1))
+        new = p_step([kept[c] for c in range(3)], here, [nx, bar[0, inner, 8 + NY, :], bar[0, after, 7 + NY, :]],
+                     [bar[1 + c, inner, 7 + NY, :] for c in range(3)])
+        for c in range(3):
+            p[c, inner, 7 + NY, :] = new[c]
+        v = [bar[1 + c, inner, 8, :] for c in range(3)]
+        bx = [jnp.where(first, kept[10 + c], lanes(v[c], 1)) for c in range(3)]
+        new = q_step([kept[3 + i] for i in range(6)], v,
+                     [bx, [bar[1 + c, inner, 7, :] for c in range(3)], [bar[1 + c, before, 8, :] for c in range(3)]])
+        for i in range(6):
+            q[i, before, 0, :] = new[i]
+
+    def y_layers(r):
+        bar = bars[r]
         here = bar[0, inner, 7, :]
-        row = jnp.broadcast_to(d_xpym[r, 0, 7:8, :], (8, 128))
-        col = jnp.sum(jnp.where(lane == 8 * sub + 6, row, 0.0), axis=1, keepdims=True)
-        nx = jnp.where(lane < 127, lanes(here, -1), jnp.where(up[0], jnp.broadcast_to(col, (8, 128)), here))
+        nx = jnp.where(lane < 127, lanes(here, -1), jnp.where(up[0], low_column(d_xpym.at[r]), here))
         new = p_step([p[c, inner, 7, :] for c in range(3)], here,
                      [nx, bar[0, inner, 8, :], bar[0, after, 7, :]], [bar[1 + c, inner, 7, :] for c in range(3)])
         new[1] = jnp.where(down[1], new[1], zero)
@@ -345,21 +380,17 @@
             p[c, inner, 7, :] = new[c]
 
         v = [bar[1 + c, inner, 8 + NY, :] for c in range(3)]
-        bx = []
-        for c in range(3):
-            f = 1 + c
-            row = jnp.broadcast_to(d_xmyp[r, f // 2, 0:1, :], (8, 128))
-            source = lax.rem(8 * sub + (f % 2) * 64 + 127, 128)
-            col = jnp.sum(jnp.where(lane == source, row, 0.0), axis=1, keepdims=True)
-            bx.append(jnp.where(lane > 0, lanes(v[c], 1),
-                                jnp.where(down[0], jnp.broadcast_to(col, (8, 128)), v[c])))
+        bx = [jnp.where(lane > 0, lanes(v[c], 1), jnp.where(down[0], high_column(d_xmyp.at[r], 1 + c), v[c]))
+              for c in range(3)]
         new = q_step([q[i, before, NY, :] for i in range(6)], v,
                      [bx, [bar[1 + c, inner, 7 + NY, :] for c in range(3)],
                       [bar[1 + c, before, 8 + NY, :] for c in range(3)]])
         for i in range(6):
             q[i, before, NY, :] = jnp.where(up[1], new[i], zero) if i in Q_OF[1] else new[i]
 
-        for t in EVERY:
+    def z_layers(r, tiles):
+        bar = bars[r]
+        for t in tiles:
             rows = slice(8 + 8 * t, 16 + 8 * t)
             here = bar[0, 0, rows, :]
             nx = jnp.where(lane < 127, lanes(here, -1),
@@ -380,7 +411,6 @@
                           [bar[1 + c, NZ, rows, :] for c in range(3)]])
             for i in range(6):
                 q[i, NZ, 8 * t : 8 * t + 8, :] = jnp.where(up[2], new[i], zero) if i in Q_OF[2] else new[i]
-        return below_x, above_x
 
     def dual(r, tiles):
         bar = bars[r]
@@ -394,15 +424,16 @@
                 here = bar[0, z + 1, rows, :]
                 v = [bar[1 + c, z + 1, rows, :] for c in range(3)]
                 nx = jnp.where(last, lanes(high, 127 - 2 * s), lanes(here, -1))
+                ny = subs(here, -1) if t == TILES - 1 else bar[0, z + 1, 9 + 8 * t : 17 + 8 * t, :]
+                by = [subs(v[c], 1) if t == 0 else bar[1 + c, z + 1, 7 + 8 * t : 15 + 8 * t, :] for c in range(3)]
                 new = p_step([p[c, z + 1, rows, :] for c in range(3)], here,
-                             [nx, bar[0, z + 1, 9 + 8 * t : 17 + 8 * t, :], bar[0, z + 2, rows, :]], v)
+                             [nx, ny, bar[0, z + 2, rows, :]], v)
                 for c in range(3):
                     p[c, z + 1, rows, :] = new[c]
                 bx = [jnp.where(first, lanes(low[(1 + c) // 2], 1 - ((1 + c) % 2) * 64 - 2 * s), lanes(v[c], 1))
                       for c in range(3)]
                 new = q_step([q[i, z, mine, :] for i in range(6)], v,
-                             [bx, [bar[1 + c, z + 1, 7 + 8 * t : 15 + 8 * t, :] for c in range(3)],
-                              [bar[1 + c, z, rows, :] for c in range(3)]])
+                             [bx, by, [bar[1 + c, z, rows, :] for c in range(3)]])
                 for i in range(6):
                     q[i, z, mine, :] = new[i]
 
@@ -418,8 +449,10 @@
                 new, values = primal_tile(z, t, masks, p, q, old, (fa[z, mine, :], wb[z, mine, :]), below_x, above_x)
                 for f in range(4):
                     uv[f, z, mine, :] = new[f]
-                    bars[r + 1][f, z + 1, rows, :] = values[f]
-                pack_into(acc, z, t, values, edge, 0)
+                    if r < ITERS - 1:
+                        bars[r + 1][f, z + 1, rows, :] = values[f]
+                if r < ITERS - 1:
+                    pack_into(acc, z, t, values, edge, 0)
 
     for r in range(ITERS):
         receive(r, NEAR0 if r == 0 else NEAR)
@@ -429,20 +462,22 @@
                 plx[c] = lanes(plxk[c // 2], (c % 2) * 64)
             for i in range(6):
                 qux[i] = lanes(quxk[i // 2], (i % 2) * 64)
-        dual(r, INNER)
+        keep_rows(r)
+        dual(r, EVERY)
+        z_layers(r, INNER)
+        acc = [zero, zero]
+        primal(r, INNER, acc, *x_layers(r, False))
         receive(r, FAR0 if r == 0 else FAR)
         clamp_far(r)
-        below_x, above_x = layers(r)
-        dual(r, OUTER)
+        below_x, above_x = x_layers(r, True)
+        y_layers(r)
+        z_layers(r, OUTER)
+        redo_rows(r)
         if r < ITERS - 1:
-            acc = [zero, zero]
             primal(r, OUTER, acc, below_x, above_x)
             for h in range(2):
-                xey[r + 1, h] = acc[h]
+                xe[r + 1, h] = acc[h]
             send(r + 1, FAR)
-            primal(r, INNER, acc, below_x, above_x)
-            for h in range(2):
-                xe[r + 1, h] = acc[h]
             send(r + 1, NEAR)
     cols[0] = below_x
     for j in range(3):
@@ -463,24 +498,30 @@
     ]
     for c in stores:
         c.start()
+    middle = slice(8, NY - 8)
+    more = [
+        pltpu.make_async_copy(uv.at[0, :, middle, :], u_out.at[:, middle, :], out_sem.at[2]),
+        pltpu.make_async_copy(uv.at[1:4, :, middle, :], v_out.at[:, :, middle, :], out_sem.at[3]),
+    ]
+    for c in more:
+        c.start()
+    stores += more
     below_x = cols[0]
     above_x = [cols[1 + j] for j in range(3)]
-    for z in range(NZ):
-        for t in EVERY:
-            mine = slice(8 * t, 8 * t + 8)
+    for k, t in enumerate(OUTER):
+        mine = slice(8 * t, 8 * t + 8)
+        for z in range(NZ):
             new, _ = primal_tile(z, t, masks, p, q, [uv[f, z, mine, :] for f in range(4)],
                                  (fa[z, mine, :], wb[z, mine, :]), below_x, above_x)
             for f in range(4):
-                new_uv[f, z, mine, :] = new[f]
-        if z % 4 == 3:
-            part = slice(z - 3, z + 1)
-            more = [
-                pltpu.make_async_copy(new_uv.at[0, part], u_out.at[part], out_sem.at[2 + z // 4]),
-                pltpu.make_async_copy(new_uv.at[1:4, part], v_out.at[:, part], out_sem.at[4 + z // 4]),
-            ]
-            for c in more:
-                c.start()
-            stores += more
+                new_uv[k, f, z] = new[f]
+        more = [
+            pltpu.make_async_copy(new_uv.at[k, 0], u_out.at[:, mine, :], out_sem.at[4 + k]),
+            pltpu.make_async_copy(new_uv.at[k, 1:4], v_out.at[:, :, mine, :], out_sem.at[6 + k]),
+        ]
+        for c in more:
+            c.start()
+        stores += more
     for c in stores:
         c.wait()
 
@@ -507,7 +548,7 @@
         out_specs=(here,) * 6,
         scratch_shapes=[
             vmem(4, NZ + 2, ROWS, NX), vmem(4, NZ + 2, ROWS, NX), vmem(4, NZ + 2, ROWS, NX),
-            vmem(ITERS, 2, *tile), vmem(ITERS, 2, *tile),
+            vmem(ITERS, 2, *tile), vmem(13, *tile),
             vmem(ITERS, 2, *tile), vmem(ITERS, 2, *tile),
             vmem(ITERS, 2, *tile), vmem(ITERS, 2, *tile), vmem(ITERS, 2, *tile), vmem(ITERS, 2, *tile),
             vmem(2, *tile), vmem(3, *tile), vmem(2, *tile), vmem(3, *tile),
@@ -527,7 +568,7 @@
                         ((NZ, NY, NX), (3, NZ, NY, NX), (3, NZ, NY, NX), (6, NZ, NY, NX))),
         in_specs=[here] * 6,
         out_specs=(hbm,) * 4,
-        scratch_shapes=[vmem(4, NZ, NY, NX), pltpu.SemaphoreType.DMA((6,))],
+        scratch_shapes=[vmem(2, 4, NZ, *tile), pltpu.SemaphoreType.DMA((8,))],
         compiler_params=pltpu.CompilerParams(vmem_limit_bytes=24 << 20),
         name="tgv_last",
     )(*state)

time: 25.2 us -> 23.9 us (0.948)
  Pallas kernels: 24.4 us -> 23.1 us
    pallas_call x1, Pallas kernels: 23.1 us -> 21.9 us  [per_device(): pl.pallas_call(functools.partial(exchange_kernel, sizes), out_shape=(vmem...]
where the time goes in v3:
time: 23.9 us; the launch traced here: 23.8 us
  Pallas kernels  23.1 us (97%)
  between operations  0.64 us (3%)
    pallas_call x1, Pallas kernels, per_device(): pl.pallas_call(functools.partial(exchange_kernel, sizes), out_shape=(vmem...  21.9 us
    pallas_call x1, Pallas kernels, per_device(): pl.pallas_call(functools.partial(final_kernel, sizes), out_shape=tuple((j...  1.24 us

profile of v3, /device:TPU:7, one launch (start us, length us, event | category | flops | bytes accessed | tf_op | source)
XLA Modules:
  0.0 23.8 jit_solution(3953996916983146629)
XLA Ops:
  0.6 21.9 %tgv_rounds.1 = (f32[4,8,32,128]{3,2,1,0:T(8,128)S(1)}, f32[3,9,40,128]{3,2,1,0:T(8,128)S(1)}, f32[6,9,40,128]{3,2,1,0:T(8,128)S(1)}, f32[8,32,128]{2,1,0:T(8,12...) custom-call(f32[8,32,128]{2,1,0:T(8,128)} %f_in.1, f32[8,32,128]{2,1,0:T(8,128)} %w_in.1, ...), custom_call_target="tpu_custom_call" | custom-call | tf_op jit(solution)/shard_map/tgv_rounds/pallas_call | solution.py:537
  22.5 1.2 %tgv_last.1 = (f32[8,32,128]{2,1,0:T(8,128)}, f32[3,8,32,128]{3,2,1,0:T(8,128)}, f32[3,8,32,128]{3,2,1,0:T(8,128)}, f32[6,8,32,128]{3,2,1,0:T(8,128)}) custom-call(f32[4,8,32,128]{3,2,1,0:T(8,128)S(1)} %get-tuple-element.10.uv, f32[3,9,40,128]{3,2,1,0:T(8,128)S(1)} %get-tuple-element.11.p, f32[6,9,40,128]{3,2,1,0:T(8,128)S(1)} %get-tuple-element.12.q, ...), custom_call_target="tpu_custom_call" | custom-call | tf_op jit(solution)/shard_map/tgv_last/pallas_call | solution.py:565

commit v4 on v3

--- a/solution.py
+++ b/solution.py
@@ -29,10 +29,14 @@
     PZ: (0, 0, 1), QZ: (0, 0, -1), PY: (0, 1, 0), QY: (0, -1, 0), PX_: (1, 0, 0), QX_: (-1, 0, 0),
 }
 N_BAR = 12
-FAR = (XUP_YDN, XDN_YUP, YUP, YDN, YUP_ZDN, YDN_ZUP)
-NEAR = (ZDN, ZUP, XUP, XDN, XUP_ZDN, XDN_ZUP)
-FAR0 = FAR + (QY, PY)
-NEAR0 = NEAR + (QZ, PZ, PX_, QX_)
+LOWER = (XDN_YUP, YUP, YUP_ZDN)
+UPPER = (XUP_YDN, YDN, YDN_ZUP)
+ALONG_X = (XUP, XDN)
+ALONG_Z = (XUP_ZDN, XDN_ZUP, ZDN, ZUP)
+LOWER0, UPPER0 = LOWER + (PY,), UPPER + (QY,)
+ALONG_X0, ALONG_Z0 = ALONG_X + (PX_, QX_), ALONG_Z + (QZ, PZ)
+ALL = LOWER + UPPER + ALONG_X + ALONG_Z
+ALL0 = LOWER0 + UPPER0 + ALONG_X0 + ALONG_Z0
 INNER = tuple(range(1, TILES - 1))
 OUTER = (0, TILES - 1)
 EVERY = tuple(range(TILES))
@@ -62,6 +66,19 @@
 
 def subs(x, by):
     return pltpu.roll(x, by % 8, 0)
+
+
+def flat(ref):
+    fields, slabs, rows, columns = ref.shape
+    return ref.reshape(fields, slabs * rows, columns)
+
+
+def steps(ref, slab, row):
+    return pl.ds(slab * ref.shape[2] + row, NZ, stride=ref.shape[2])
+
+
+def line(ref, field, slab, row):
+    return flat(ref)[field, steps(ref, slab, row), :]
 
 
 def tile_iota(axis):
@@ -111,7 +128,7 @@
 
 def exchange_kernel(sizes, f_in, w_in, u_in, v_in, p_in, q_in,
                     uv, p, q, fa, wb, cols,
-                    bar0, bar1, bar2, xe, kept, xh_lo, xh_hi, d_xmyp, d_xpym, d_xmzp, d_xpzm,
+                    bar0, bar1, bar2, xe, xey, xei, kept, xh_lo, xh_hi, d_xmyp, d_xpym, d_xmzp, d_xpzm,
                     pxk, qxk, plxk, quxk, plx, qux,
                     in_sem, send_sem, recv_sem):
     at, up, down = place(sizes)
@@ -141,7 +158,7 @@
     ]
     barrier = pltpu.get_barrier_semaphore()
     arrivals = jnp.int32(0)
-    for m in FAR + NEAR:
+    for m in ALL:
         move = MOVES[m]
         arrivals = arrivals + exists(move).astype(jnp.int32)
 
@@ -178,9 +195,9 @@
         if m == QY:
             return q_in.at[:, :, 0, :], q.at[:, 0:NZ, NY, :]
         if m == XUP_YDN:
-            return xe.at[r, :, 0, :], d_xmyp.at[r, :, 0, :]
+            return xey.at[r, 0, :, 0, :], d_xmyp.at[r, :, 0, :]
         if m == XDN_YUP:
-            return xe.at[r, :, 7, :], d_xpym.at[r, :, 7, :]
+            return xey.at[r, 1, :, 7, :], d_xpym.at[r, :, 7, :]
         if m == PX_:
             return pxk, plxk
         if m == QX_:
@@ -228,6 +245,8 @@
             pack_into(acc, z, t, [bar0[f, z + 1, 8 + 8 * t : 16 + 8 * t, :] for f in range(4)], edge, 0)
     for h in range(2):
         xe[0, h] = acc[h]
+        xey[0, 0, h] = acc[h]
+        xey[0, 1, h] = acc[h]
     loads[2].wait()
     loads[3].wait()
     accp, accq = [zero, zero], [zero, zero, zero]
@@ -241,8 +260,7 @@
         qxk[h] = accq[h]
 
     pl.semaphore_wait(barrier, arrivals)
-    send(0, FAR0)
-    send(0, NEAR0)
+    send(0, ALL0)
 
     loads[4].wait()
     loads[5].wait()
@@ -256,9 +274,7 @@
     def split(x):
         return [x[0], lanes(x[0], 64), x[1], lanes(x[1], 64)]
 
-    def clamp_near(r):
-        bar = bars[r]
-
+    def clamp_x(r):
         @pl.when(jnp.logical_not(up[0]))
         def _():
             for h in range(2):
@@ -269,6 +285,9 @@
             for h in range(2):
                 xh_lo[r, h] = lanes(xe[r, h], -1)
 
+    def clamp_z(r):
+        bar = bars[r]
+
         @pl.when(jnp.logical_not(up[2]))
         def _():
             bar[:, NZ + 1, 8 : 8 + NY, :] = bar[:, NZ, 8 : 8 + NY, :]
@@ -277,7 +296,7 @@
         def _():
             bar[:, 0, 8 : 8 + NY, :] = bar[:, 1, 8 : 8 + NY, :]
 
-    def clamp_far(r):
+    def clamp_lower(r):
         bar = bars[r]
 
         @pl.when(jnp.logical_not(up[2]))
@@ -285,6 +304,15 @@
             for f in range(4):
                 bar[f, NZ + 1, 7:8, :] = bar[f, NZ, 7:8, :]
 
+        @pl.when(jnp.logical_not(down[1]))
+        def _():
+            for f in range(4):
+                bar[f, NZ + 1, 7:8, :] = bar[f, NZ + 1, 8:9, :]
+                flat(bar)[f, steps(bar, 1, 7), :] = line(bar, f, 1, 8)
+
+    def clamp_upper(r):
+        bar = bars[r]
+
         @pl.when(jnp.logical_not(down[2]))
         def _():
             for f in range(4):
@@ -294,32 +322,26 @@
         def _():
             for f in range(4):
                 bar[f, 0, 8 + NY : 9 + NY, :] = bar[f, 0, 7 + NY : 8 + NY, :]
-                bar[f, 1 : NZ + 1, 8 + NY, :] = bar[f, 1 : NZ + 1, 7 + NY, :]
-
-        @pl.when(jnp.logical_not(down[1]))
-        def _():
-            for f in range(4):
-                bar[f, NZ + 1, 7:8, :] = bar[f, NZ + 1, 8:9, :]
-                bar[f, 1 : NZ + 1, 7, :] = bar[f, 1 : NZ + 1, 8, :]
+                flat(bar)[f, steps(bar, 1, 8 + NY), :] = line(bar, f, 1, 7 + NY)
 
     in64 = lax.rem(lane, 64)
     in8 = lax.rem(lane, 8)
 
-    def x_layers(r, corners):
-        own = [xe[r, h] for h in range(2)]
-        own_high = [lanes(x, 1) for x in own]
+    def x_below(r, corners):
         low = [lanes(xh_lo[r, h], 1) for h in range(2)]
         here = low[0]
         a = subs(here, -1)
         corner = jnp.where(up[1], lanes(subs(d_xmyp[r, 0], -1), 7), here) if corners else here
         ny = jnp.where(sub < 7, a, jnp.where(in8 < 6, lanes(a, -2), corner))
         nz = jnp.where(in64 < 56, lanes(here, -8), jnp.where(up[2], lanes(d_xmzp[r, 0], 57), here))
-        new = p_step([plx[c] for c in range(3)], here, [own[0], ny, nz], split(low)[1:])
+        new = p_step([plx[c] for c in range(3)], here, [xe[r, 0], ny, nz], split(low)[1:])
         if corners:
             for c in range(3):
                 plx[c] = new[c]
-        below_x = jnp.where(down[0], new[0], zero)
-
+        return jnp.where(down[0], new[0], zero)
+
+    def x_above(r, corners):
+        own_high = [lanes(xe[r, h], 1) for h in range(2)]
         high = [xh_hi[r, h] for h in range(2)]
         py_, pz_ = [], []
         for h in range(2):
@@ -333,7 +355,7 @@
         if corners:
             for i in range(6):
                 qux[i] = new[i]
-        return below_x, [jnp.where(up[0], new[i], zero) for i in Q_OF[0]]
+        return [jnp.where(up[0], new[i], zero) for i in Q_OF[0]]
 
     def high_column(source, f):
         row = jnp.broadcast_to(source[f // 2, 0:1, :], (8, 128))
@@ -344,51 +366,55 @@
         row = jnp.broadcast_to(source[0, 7:8, :], (8, 128))
         return jnp.broadcast_to(jnp.sum(jnp.where(lane == 8 * sub + 6, row, 0.0), axis=1, keepdims=True), (8, 128))
 
-    inner, after, before = slice(1, NZ + 1), slice(2, NZ + 2), slice(0, NZ)
 
     def keep_rows(r):
         for c in range(3):
-            kept[c] = p[c, inner, 7 + NY, :]
+            kept[c] = line(p, c, 1, 7 + NY)
             kept[10 + c] = high_column(xh_lo.at[r], 1 + c)
         for i in range(6):
-            kept[3 + i] = q[i, before, 0, :]
+            kept[3 + i] = line(q, i, 0, 0)
         kept[9] = low_column(xh_hi.at[r])
 
-    def redo_rows(r):
-        bar = bars[r]
-        here = bar[0, inner, 7 + NY, :]
+    def redo_upper(r):
+        bar = bars[r]
+        here = line(bar, 0, 1, 7 + NY)
         nx = jnp.where(last, kept[9], lanes(here, -1))
-        new = p_step([kept[c] for c in range(3)], here, [nx, bar[0, inner, 8 + NY, :], bar[0, after, 7 + NY, :]],
-                     [bar[1 + c, inner, 7 + NY, :] for c in range(3)])
+        new = p_step([kept[c] for c in range(3)], here, [nx, line(bar, 0, 1, 8 + NY), line(bar, 0, 2, 7 + NY)],
+                     [line(bar, 1 + c, 1, 7 + NY) for c in range(3)])
         for c in range(3):
-            p[c, inner, 7 + NY, :] = new[c]
-        v = [bar[1 + c, inner, 8, :] for c in range(3)]
+            flat(p)[c, steps(p, 1, 7 + NY), :] = new[c]
+
+    def redo_lower(r):
+        bar = bars[r]
+        v = [line(bar, 1 + c, 1, 8) for c in range(3)]
         bx = [jnp.where(first, kept[10 + c], lanes(v[c], 1)) for c in range(3)]
         new = q_step([kept[3 + i] for i in range(6)], v,
-                     [bx, [bar[1 + c, inner, 7, :] for c in range(3)], [bar[1 + c, before, 8, :] for c in range(3)]])
+                     [bx, [line(bar, 1 + c, 1, 7) for c in range(3)], [line(bar, 1 + c, 0, 8) for c in range(3)]])
         for i in range(6):
-            q[i, before, 0, :] = new[i]
-
-    def y_layers(r):
-        bar = bars[r]
-        here = bar[0, inner, 7, :]
+            flat(q)[i, steps(q, 0, 0), :] = new[i]
+
+    def y_below(r):
+        bar = bars[r]
+        here = line(bar, 0, 1, 7)
         nx = jnp.where(lane < 127, lanes(here, -1), jnp.where(up[0], low_column(d_xpym.at[r]), here))
-        new = p_step([p[c, inner, 7, :] for c in range(3)], here,
-                     [nx, bar[0, inner, 8, :], bar[0, after, 7, :]], [bar[1 + c, inner, 7, :] for c in range(3)])
+        new = p_step([line(p, c, 1, 7) for c in range(3)], here,
+                     [nx, line(bar, 0, 1, 8), line(bar, 0, 2, 7)], [line(bar, 1 + c, 1, 7) for c in range(3)])
         new[1] = jnp.where(down[1], new[1], zero)
         for c in range(3):
-            p[c, inner, 7, :] = new[c]
-
-        v = [bar[1 + c, inner, 8 + NY, :] for c in range(3)]
+            flat(p)[c, steps(p, 1, 7), :] = new[c]
+
+    def y_above(r):
+        bar = bars[r]
+        v = [line(bar, 1 + c, 1, 8 + NY) for c in range(3)]
         bx = [jnp.where(lane > 0, lanes(v[c], 1), jnp.where(down[0], high_column(d_xmyp.at[r], 1 + c), v[c]))
               for c in range(3)]
-        new = q_step([q[i, before, NY, :] for i in range(6)], v,
-                     [bx, [bar[1 + c, inner, 7 + NY, :] for c in range(3)],
-                      [bar[1 + c, before, 8 + NY, :] for c in range(3)]])
+        new = q_step([line(q, i, 0, NY) for i in range(6)], v,
+                     [bx, [line(bar, 1 + c, 1, 7 + NY) for c in range(3)],
+                      [line(bar, 1 + c, 0, 8 + NY) for c in range(3)]])
         for i in range(6):
-            q[i, before, NY, :] = jnp.where(up[1], new[i], zero) if i in Q_OF[1] else new[i]
-
-    def z_layers(r, tiles):
+            flat(q)[i, steps(q, 0, NY), :] = jnp.where(up[1], new[i], zero) if i in Q_OF[1] else new[i]
+
+    def z_below(r, tiles):
         bar = bars[r]
         for t in tiles:
             rows = slice(8 + 8 * t, 16 + 8 * t)
@@ -402,6 +428,10 @@
             for c in range(3):
                 p[c, 0, rows, :] = new[c]
 
+    def z_above(r, tiles):
+        bar = bars[r]
+        for t in tiles:
+            rows = slice(8 + 8 * t, 16 + 8 * t)
             v = [bar[1 + c, NZ + 1, rows, :] for c in range(3)]
             bx = [jnp.where(lane > 0, lanes(v[c], 1),
                             jnp.where(down[0], lanes(d_xmzp[r, (1 + c) // 2], -((1 + c) % 2) * 64 - 2 * t + 1), v[c]))
@@ -412,12 +442,12 @@
             for i in range(6):
                 q[i, NZ, 8 * t : 8 * t + 8, :] = jnp.where(up[2], new[i], zero) if i in Q_OF[2] else new[i]
 
-    def dual(r, tiles):
+    def dual(r, slabs):
         bar = bars[r]
         high = xh_hi[r, 0]
         low = [xh_lo[r, h] for h in range(2)]
-        for t in tiles:
-            for z in range(NZ):
+        for z in slabs:
+            for t in EVERY:
                 rows = slice(8 + 8 * t, 16 + 8 * t)
                 mine = slice(8 * t, 8 * t + 8)
                 s = z * TILES + t
@@ -454,36 +484,80 @@
                 if r < ITERS - 1:
                     pack_into(acc, z, t, values, edge, 0)
 
+    low_side = at[1] < sizes[1] // 2
     for r in range(ITERS):
-        receive(r, NEAR0 if r == 0 else NEAR)
-        clamp_near(r)
-        if r == 0:
+        start, more = r == 0, r < ITERS - 1
+        receive(r, ALONG_X0 if start else ALONG_X)
+        clamp_x(r)
+        if start:
             for c in range(3):
                 plx[c] = lanes(plxk[c // 2], (c % 2) * 64)
             for i in range(6):
                 qux[i] = lanes(quxk[i // 2], (i % 2) * 64)
         keep_rows(r)
-        dual(r, EVERY)
-        z_layers(r, INNER)
+        dual(r, range(1, NZ - 1))
+        receive(r, ALONG_Z0 if start else ALONG_Z)
+        clamp_z(r)
+        dual(r, (0, NZ - 1))
+        z_below(r, EVERY[:-1])
+        z_above(r, EVERY[1:])
+        below_x, above_x = x_below(r, False), x_above(r, False)
         acc = [zero, zero]
-        primal(r, INNER, acc, *x_layers(r, False))
-        receive(r, FAR0 if r == 0 else FAR)
-        clamp_far(r)
-        below_x, above_x = x_layers(r, True)
-        y_layers(r)
-        z_layers(r, OUTER)
-        redo_rows(r)
-        if r < ITERS - 1:
-            primal(r, OUTER, acc, below_x, above_x)
+        primal(r, INNER, acc, below_x, above_x)
+        for h in range(2):
+            xei[h] = acc[h]
+        cols[0] = below_x
+        for j in range(3):
+            cols[1 + j] = above_x[j]
+
+        def border(t, below, above, side, sends):
+            acc = [zero, zero]
+            primal(r, (t,), acc, below, above)
             for h in range(2):
-                xe[r + 1, h] = acc[h]
-            send(r + 1, FAR)
-            send(r + 1, NEAR)
-    cols[0] = below_x
-    for j in range(3):
-        cols[1 + j] = above_x[j]
+                xey[r + 1, side, h] = acc[h]
+            send(r + 1, sends)
+
+        def lower():
+            receive(r, LOWER0 if start else LOWER)
+            clamp_lower(r)
+            above = x_above(r, True)
+            y_below(r)
+            z_above(r, (0,))
+            redo_lower(r)
+            if more:
+                border(0, cols[0], above, 0, UPPER)
+            else:
+                for j in range(3):
+                    cols[4 + j] = above[j]
+
+        def upper():
+            receive(r, UPPER0 if start else UPPER)
+            clamp_upper(r)
+            below = x_below(r, True)
+            y_above(r)
+            z_below(r, (TILES - 1,))
+            redo_upper(r)
+            if more:
+                border(TILES - 1, below, [cols[1 + j] for j in range(3)], 1, LOWER)
+            else:
+                cols[7] = below
+
+        @pl.when(low_side)
+        def _():
+            lower()
+            upper()
+
+        @pl.when(jnp.logical_not(low_side))
+        def _():
+            upper()
+            lower()
+
+        if more:
+            for h in range(2):
+                xe[r + 1, h] = xei[h] + (xey[r + 1, 0, h] + xey[r + 1, 1, h])
+            send(r + 1, ALONG_X + ALONG_Z)
     for r in range(ITERS):
-        for m in (FAR0 + NEAR0 if r == 0 else FAR + NEAR):
+        for m in (ALL0 if r == 0 else ALL):
             @pl.when(exists(MOVES[m]))
             def _():
                 message(m, r).wait_send()
@@ -506,13 +580,12 @@
     for c in more:
         c.start()
     stores += more
-    below_x = cols[0]
-    above_x = [cols[1 + j] for j in range(3)]
     for k, t in enumerate(OUTER):
         mine = slice(8 * t, 8 * t + 8)
         for z in range(NZ):
             new, _ = primal_tile(z, t, masks, p, q, [uv[f, z, mine, :] for f in range(4)],
-                                 (fa[z, mine, :], wb[z, mine, :]), below_x, above_x)
+                                 (fa[z, mine, :], wb[z, mine, :]), cols[7 * k],
+                                 [cols[4 - 3 * k + j] for j in range(3)])
             for f in range(4):
                 new_uv[k, f, z] = new[f]
         more = [
@@ -542,13 +615,13 @@
             vmem(6, NZ + 1, PROWS, NX),
             vmem(NZ, NY, NX),
             vmem(NZ, NY, NX),
-            vmem(4, *tile),
+            vmem(8, *tile),
         ),
         in_specs=[hbm] * 6,
         out_specs=(here,) * 6,
         scratch_shapes=[
             vmem(4, NZ + 2, ROWS, NX), vmem(4, NZ + 2, ROWS, NX), vmem(4, NZ + 2, ROWS, NX),
-            vmem(ITERS, 2, *tile), vmem(13, *tile),
+            vmem(ITERS, 2, *tile), vmem(ITERS, 2, 2, *tile), vmem(2, *tile), vmem(13, *tile),
             vmem(ITERS, 2, *tile), vmem(ITERS, 2, *tile),
             vmem(ITERS, 2, *tile), vmem(ITERS, 2, *tile), vmem(ITERS, 2, *tile), vmem(ITERS, 2, *tile),
             vmem(2, *tile), vmem(3, *tile), vmem(2, *tile), vmem(3, *tile),

time: 23.9 us -> 23 us (0.962)
  Pallas kernels: 23.1 us -> 22.2 us
    pallas_call x1, Pallas kernels: 21.9 us -> 21 us  [per_device(): pl.pallas_call(functools.partial(exchange_kernel, sizes), out_shape=(vmem...]
where the time goes in v4:
time: 23 us; the launch traced here: 22.9 us
  Pallas kernels  22.2 us (97%)
  between operations  0.64 us (3%)
    pallas_call x1, Pallas kernels, per_device(): pl.pallas_call(functools.partial(exchange_kernel, sizes), out_shape=(vmem...  21 us
    pallas_call x1, Pallas kernels, per_device(): pl.pallas_call(functools.partial(final_kernel, sizes), out_shape=tuple((j...  1.24 us

profile of v4, /device:TPU:7, one launch (start us, length us, event | category | flops | bytes accessed | tf_op | source)
XLA Modules:
  0.0 22.9 jit_solution(14140293107281162972)
XLA Ops:
  0.6 21.0 %tgv_rounds.1 = (f32[4,8,32,128]{3,2,1,0:T(8,128)S(1)}, f32[3,9,40,128]{3,2,1,0:T(8,128)S(1)}, f32[6,9,40,128]{3,2,1,0:T(8,128)S(1)}, f32[8,32,128]{2,1,0:T(8,12...) custom-call(f32[8,32,128]{2,1,0:T(8,128)} %f_in.1, f32[8,32,128]{2,1,0:T(8,128)} %w_in.1, ...), custom_call_target="tpu_custom_call" | custom-call | tf_op jit(solution)/shard_map/tgv_rounds/pallas_call | solution.py:610
  21.6 1.2 %tgv_last.1 = (f32[8,32,128]{2,1,0:T(8,128)}, f32[3,8,32,128]{3,2,1,0:T(8,128)}, f32[3,8,32,128]{3,2,1,0:T(8,128)}, f32[6,8,32,128]{3,2,1,0:T(8,128)}) custom-call(f32[4,8,32,128]{3,2,1,0:T(8,128)S(1)} %get-tuple-element.10.uv, f32[3,9,40,128]{3,2,1,0:T(8,128)S(1)} %get-tuple-element.11.p, f32[6,9,40,128]{3,2,1,0:T(8,128)S(1)} %get-tuple-element.12.q, ...), custom_call_target="tpu_custom_call" | custom-call | tf_op jit(solution)/shard_map/tgv_last/pallas_call | solution.py:638

commit v5 on v4

--- a/solution.py
+++ b/solution.py
@@ -37,6 +37,7 @@
 ALONG_X0, ALONG_Z0 = ALONG_X + (PX_, QX_), ALONG_Z + (QZ, PZ)
 ALL = LOWER + UPPER + ALONG_X + ALONG_Z
 ALL0 = LOWER0 + UPPER0 + ALONG_X0 + ALONG_Z0
+CORNER = (7, -6)
 INNER = tuple(range(1, TILES - 1))
 OUTER = (0, TILES - 1)
 EVERY = tuple(range(TILES))
@@ -129,7 +130,7 @@
 def exchange_kernel(sizes, f_in, w_in, u_in, v_in, p_in, q_in,
                     uv, p, q, fa, wb, cols,
                     bar0, bar1, bar2, xe, xey, xei, kept, xh_lo, xh_hi, d_xmyp, d_xpym, d_xmzp, d_xpzm,
-                    pxk, qxk, plxk, quxk, plx, qux,
+                    pxk, qxk, pyk, qyk, pzk, qzk, plxk, quxk, plx, qux,
                     in_sem, send_sem, recv_sem):
     at, up, down = place(sizes)
     bars = (bar0, bar1, bar2)
@@ -187,17 +188,17 @@
         if m == YDN_ZUP:
             return bar.at[:, NZ, 8, :], bar.at[:, 0, 8 + NY, :]
         if m == PZ:
-            return p_in.at[:, NZ - 1, :, :], p.at[:, 0, 8 : 8 + NY, :]
+            return pzk, p.at[:, 0, 8 : 8 + NY, :]
         if m == QZ:
-            return q_in.at[:, 0, :, :], q.at[:, NZ, 0:NY, :]
+            return qzk, q.at[:, NZ, 0:NY, :]
         if m == PY:
-            return p_in.at[:, :, NY - 1, :], p.at[:, 1 : NZ + 1, 7, :]
+            return pyk, p.at[:, 1 : NZ + 1, 7, :]
         if m == QY:
-            return q_in.at[:, :, 0, :], q.at[:, 0:NZ, NY, :]
+            return qyk, q.at[:, 0:NZ, NY, :]
         if m == XUP_YDN:
-            return xey.at[r, 0, :, 0, :], d_xmyp.at[r, :, 0, :]
+            return xey.at[r, 0, :, 0, :], d_xmyp.at[r, :, 7, :]
         if m == XDN_YUP:
-            return xey.at[r, 1, :, 7, :], d_xpym.at[r, :, 7, :]
+            return xey.at[r, 1, :, 7, :], d_xpym.at[r, :, 0, :]
         if m == PX_:
             return pxk, plxk
         if m == QX_:
@@ -221,6 +222,12 @@
             def _():
                 message(m, r).start()
 
+    def sent(r):
+        for m in ALL0 if r == 0 else ALL:
+            @pl.when(exists(MOVES[m]))
+            def _():
+                message(m, r).wait_send()
+
     def receive(r, which):
         for m in which:
             @pl.when(exists(opposite(MOVES[m])))
@@ -245,10 +252,16 @@
             pack_into(acc, z, t, [bar0[f, z + 1, 8 + 8 * t : 16 + 8 * t, :] for f in range(4)], edge, 0)
     for h in range(2):
         xe[0, h] = acc[h]
-        xey[0, 0, h] = acc[h]
-        xey[0, 1, h] = acc[h]
+        xey[0, 0, h] = lanes(acc[h], CORNER[0])
+        xey[0, 1, h] = lanes(acc[h], CORNER[1])
     loads[2].wait()
     loads[3].wait()
+    for c in range(3):
+        pyk[c] = line(p, c, 1, 7 + NY)
+        pzk[c] = p[c, NZ, 8 : 8 + NY, :]
+    for i in range(6):
+        qyk[i] = line(q, i, 0, 0)
+        qzk[i] = q[i, 0, 0:NY, :]
     accp, accq = [zero, zero], [zero, zero, zero]
     for t in EVERY:
         for z in range(NZ):
@@ -331,7 +344,7 @@
         low = [lanes(xh_lo[r, h], 1) for h in range(2)]
         here = low[0]
         a = subs(here, -1)
-        corner = jnp.where(up[1], lanes(subs(d_xmyp[r, 0], -1), 7), here) if corners else here
+        corner = jnp.where(up[1], d_xmyp[r, 0], here) if corners else here
         ny = jnp.where(sub < 7, a, jnp.where(in8 < 6, lanes(a, -2), corner))
         nz = jnp.where(in64 < 56, lanes(here, -8), jnp.where(up[2], lanes(d_xmzp[r, 0], 57), here))
         new = p_step([plx[c] for c in range(3)], here, [xe[r, 0], ny, nz], split(low)[1:])
@@ -346,7 +359,7 @@
         py_, pz_ = [], []
         for h in range(2):
             a = subs(high[h], 1)
-            corner = jnp.where(down[1], lanes(subs(d_xpym[r, h], 1), -6), high[h]) if corners else high[h]
+            corner = jnp.where(down[1], d_xpym[r, h], high[h]) if corners else high[h]
             py_.append(jnp.where(sub > 0, a, jnp.where(in8 >= 2, lanes(a, 2), corner)))
             pz_.append(jnp.where(in64 >= 8, lanes(high[h], 8),
                                  jnp.where(down[2], lanes(d_xpzm[r, h], -56), high[h])))
@@ -357,23 +370,18 @@
                 qux[i] = new[i]
         return [jnp.where(up[0], new[i], zero) for i in Q_OF[0]]
 
-    def high_column(source, f):
-        row = jnp.broadcast_to(source[f // 2, 0:1, :], (8, 128))
-        picked = jnp.where(lane == lax.rem(8 * sub + (f % 2) * 64 + 127, 128), row, 0.0)
+    def column(source, row, base):
+        line_ = jnp.broadcast_to(source[row : row + 1, :], (8, 128))
+        picked = jnp.where(lane == lax.rem(8 * sub + base % 128, 128), line_, 0.0)
         return jnp.broadcast_to(jnp.sum(picked, axis=1, keepdims=True), (8, 128))
-
-    def low_column(source):
-        row = jnp.broadcast_to(source[0, 7:8, :], (8, 128))
-        return jnp.broadcast_to(jnp.sum(jnp.where(lane == 8 * sub + 6, row, 0.0), axis=1, keepdims=True), (8, 128))
-
 
     def keep_rows(r):
         for c in range(3):
             kept[c] = line(p, c, 1, 7 + NY)
-            kept[10 + c] = high_column(xh_lo.at[r], 1 + c)
+            kept[10 + c] = column(xh_lo.at[r, (1 + c) // 2], 0, ((1 + c) % 2) * 64 - 1)
         for i in range(6):
             kept[3 + i] = line(q, i, 0, 0)
-        kept[9] = low_column(xh_hi.at[r])
+        kept[9] = column(xh_hi.at[r, 0], 7, 6)
 
     def redo_upper(r):
         bar = bars[r]
@@ -396,7 +404,7 @@
     def y_below(r):
         bar = bars[r]
         here = line(bar, 0, 1, 7)
-        nx = jnp.where(lane < 127, lanes(here, -1), jnp.where(up[0], low_column(d_xpym.at[r]), here))
+        nx = jnp.where(lane < 127, lanes(here, -1), jnp.where(up[0], column(d_xpym.at[r, 0], 0, 6 + CORNER[1]), here))
         new = p_step([line(p, c, 1, 7) for c in range(3)], here,
                      [nx, line(bar, 0, 1, 8), line(bar, 0, 2, 7)], [line(bar, 1 + c, 1, 7) for c in range(3)])
         new[1] = jnp.where(down[1], new[1], zero)
@@ -406,7 +414,7 @@
     def y_above(r):
         bar = bars[r]
         v = [line(bar, 1 + c, 1, 8 + NY) for c in range(3)]
-        bx = [jnp.where(lane > 0, lanes(v[c], 1), jnp.where(down[0], high_column(d_xmyp.at[r], 1 + c), v[c]))
+        bx = [jnp.where(lane > 0, lanes(v[c], 1), jnp.where(down[0], column(d_xmyp.at[r, (1 + c) // 2], 7, ((1 + c) % 2) * 64 - 1 + CORNER[0]), v[c]))
               for c in range(3)]
         new = q_step([line(q, i, 0, NY) for i in range(6)], v,
                      [bx, [line(bar, 1 + c, 1, 7 + NY) for c in range(3)],
@@ -467,7 +475,7 @@
                 for i in range(6):
                     q[i, z, mine, :] = new[i]
 
-    def primal(r, tiles, acc, below_x, above_x):
+    def primal(r, tiles, acc, below_x, above_x, by=0):
         for t in tiles:
             for z in range(NZ):
                 rows = slice(8 + 8 * t, 16 + 8 * t)
@@ -482,7 +490,7 @@
                     if r < ITERS - 1:
                         bars[r + 1][f, z + 1, rows, :] = values[f]
                 if r < ITERS - 1:
-                    pack_into(acc, z, t, values, edge, 0)
+                    pack_into(acc, z, t, values, edge, by)
 
     low_side = at[1] < sizes[1] // 2
     for r in range(ITERS):
@@ -504,6 +512,8 @@
         below_x, above_x = x_below(r, False), x_above(r, False)
         acc = [zero, zero]
         primal(r, INNER, acc, below_x, above_x)
+        if r > 0:
+            sent(r - 1)
         for h in range(2):
             xei[h] = acc[h]
         cols[0] = below_x
@@ -512,7 +522,7 @@
 
         def border(t, below, above, side, sends):
             acc = [zero, zero]
-            primal(r, (t,), acc, below, above)
+            primal(r, (t,), acc, below, above, CORNER[side])
             for h in range(2):
                 xey[r + 1, side, h] = acc[h]
             send(r + 1, sends)
@@ -554,13 +564,9 @@
 
         if more:
             for h in range(2):
-                xe[r + 1, h] = xei[h] + (xey[r + 1, 0, h] + xey[r + 1, 1, h])
+                xe[r + 1, h] = xei[h] + (lanes(xey[r + 1, 0, h], -CORNER[0]) + lanes(xey[r + 1, 1, h], -CORNER[1]))
             send(r + 1, ALONG_X + ALONG_Z)
-    for r in range(ITERS):
-        for m in (ALL0 if r == 0 else ALL):
-            @pl.when(exists(MOVES[m]))
-            def _():
-                message(m, r).wait_send()
+    sent(ITERS - 1)
 
 
 def final_kernel(sizes, uv, p, q, fa, wb, cols, u_out, v_out, p_out, q_out, new_uv, out_sem):
@@ -624,7 +630,8 @@
             vmem(ITERS, 2, *tile), vmem(ITERS, 2, 2, *tile), vmem(2, *tile), vmem(13, *tile),
             vmem(ITERS, 2, *tile), vmem(ITERS, 2, *tile),
             vmem(ITERS, 2, *tile), vmem(ITERS, 2, *tile), vmem(ITERS, 2, *tile), vmem(ITERS, 2, *tile),
-            vmem(2, *tile), vmem(3, *tile), vmem(2, *tile), vmem(3, *tile),
+            vmem(2, *tile), vmem(3, *tile), vmem(3, *tile), vmem(6, *tile), vmem(3, NY, NX), vmem(6, NY, NX),
+            vmem(2, *tile), vmem(3, *tile),
             vmem(3, *tile), vmem(6, *tile),
             pltpu.SemaphoreType.DMA((6,)),
             pltpu.SemaphoreType.DMA((ITERS, 18)),

time: 23 us -> 23 us (level)
  no operation moved by 1% of the time
where the time goes in v5:
time: 23 us; the launch traced here: 22.8 us
  Pallas kernels  22.1 us (96%)
  between operations  0.64 us (3%)
    pallas_call x1, Pallas kernels, per_device(): pl.pallas_call(functools.partial(exchange_kernel, sizes), out_shape=(vmem...  20.9 us
    pallas_call x1, Pallas kernels, per_device(): pl.pallas_call(functools.partial(final_kernel, sizes), out_shape=tuple((j...  1.24 us

profile of v5, /device:TPU:7, one launch (start us, length us, event | category | flops | bytes accessed | tf_op | source)
XLA Modules:
  0.0 22.8 jit_solution(16962587504445620935)
XLA Ops:
  0.6 20.9 %tgv_rounds.1 = (f32[4,8,32,128]{3,2,1,0:T(8,128)S(1)}, f32[3,9,40,128]{3,2,1,0:T(8,128)S(1)}, f32[6,9,40,128]{3,2,1,0:T(8,128)S(1)}, f32[8,32,128]{2,1,0:T(8,12...) custom-call(f32[8,32,128]{2,1,0:T(8,128)} %f_in.1, f32[8,32,128]{2,1,0:T(8,128)} %w_in.1, ...), custom_call_target="tpu_custom_call" | custom-call | tf_op jit(solution)/shard_map/tgv_rounds/pallas_call | solution.py:616
  21.5 1.2 %tgv_last.1 = (f32[8,32,128]{2,1,0:T(8,128)}, f32[3,8,32,128]{3,2,1,0:T(8,128)}, f32[3,8,32,128]{3,2,1,0:T(8,128)}, f32[6,8,32,128]{3,2,1,0:T(8,128)}) custom-call(f32[4,8,32,128]{3,2,1,0:T(8,128)S(1)} %get-tuple-element.10.uv, f32[3,9,40,128]{3,2,1,0:T(8,128)S(1)} %get-tuple-element.11.p, f32[6,9,40,128]{3,2,1,0:T(8,128)S(1)} %get-tuple-element.12.q, ...), custom_call_target="tpu_custom_call" | custom-call | tf_op jit(solution)/shard_map/tgv_last/pallas_call | solution.py:645

commit v6 on v5

--- a/solution.py
+++ b/solution.py
@@ -129,7 +129,7 @@
 
 def exchange_kernel(sizes, f_in, w_in, u_in, v_in, p_in, q_in,
                     uv, p, q, fa, wb, cols,
-                    bar0, bar1, bar2, xe, xey, xei, kept, xh_lo, xh_hi, d_xmyp, d_xpym, d_xmzp, d_xpzm,
+                    bar0, bar1, bar2, xe, xey, xei, kept, early, xh_lo, xh_hi, d_xmyp, d_xpym, d_xmzp, d_xpzm,
                     pxk, qxk, pyk, qyk, pzk, qzk, plxk, quxk, plx, qux,
                     in_sem, send_sem, recv_sem):
     at, up, down = place(sizes)
@@ -341,30 +341,41 @@
     in8 = lax.rem(lane, 8)
 
     def x_below(r, corners):
-        low = [lanes(xh_lo[r, h], 1) for h in range(2)]
-        here = low[0]
-        a = subs(here, -1)
-        corner = jnp.where(up[1], d_xmyp[r, 0], here) if corners else here
-        ny = jnp.where(sub < 7, a, jnp.where(in8 < 6, lanes(a, -2), corner))
-        nz = jnp.where(in64 < 56, lanes(here, -8), jnp.where(up[2], lanes(d_xmzp[r, 0], 57), here))
-        new = p_step([plx[c] for c in range(3)], here, [xe[r, 0], ny, nz], split(low)[1:])
+        if not corners:
+            low = [lanes(xh_lo[r, h], 1) for h in range(2)]
+            a = subs(low[0], -1)
+            for k, x in enumerate(split(low)):
+                early[k] = x
+            early[4] = jnp.where(sub < 7, a, jnp.where(in8 < 6, lanes(a, -2), low[0]))
+            early[5] = jnp.where(in64 < 56, lanes(low[0], -8), jnp.where(up[2], lanes(d_xmzp[r, 0], 57), low[0]))
+        ny = early[4]
+        if corners:
+            at_edge = jnp.logical_and(jnp.logical_and(sub == 7, in8 >= 6), up[1])
+            ny = jnp.where(at_edge, d_xmyp[r, 0], ny)
+        new = p_step([plx[c] for c in range(3)], early[0], [xe[r, 0], ny, early[5]], [early[1 + c] for c in range(3)])
         if corners:
             for c in range(3):
                 plx[c] = new[c]
         return jnp.where(down[0], new[0], zero)
 
     def x_above(r, corners):
-        own_high = [lanes(xe[r, h], 1) for h in range(2)]
-        high = [xh_hi[r, h] for h in range(2)]
-        py_, pz_ = [], []
-        for h in range(2):
-            a = subs(high[h], 1)
-            corner = jnp.where(down[1], d_xpym[r, h], high[h]) if corners else high[h]
-            py_.append(jnp.where(sub > 0, a, jnp.where(in8 >= 2, lanes(a, 2), corner)))
-            pz_.append(jnp.where(in64 >= 8, lanes(high[h], 8),
-                                 jnp.where(down[2], lanes(d_xpzm[r, h], -56), high[h])))
-        new = q_step([qux[i] for i in range(6)], split(high)[1:],
-                     [split(own_high)[1:], split(py_)[1:], split(pz_)[1:]])
+        if not corners:
+            high = [xh_hi[r, h] for h in range(2)]
+            py_, pz_ = [], []
+            for h in range(2):
+                a = subs(high[h], 1)
+                py_.append(jnp.where(sub > 0, a, jnp.where(in8 >= 2, lanes(a, 2), high[h])))
+                pz_.append(jnp.where(in64 >= 8, lanes(high[h], 8),
+                                     jnp.where(down[2], lanes(d_xpzm[r, h], -56), high[h])))
+            for k, x in enumerate((high, [lanes(xe[r, h], 1) for h in range(2)], py_, pz_)):
+                for c, y in enumerate(split(x)[1:]):
+                    early[6 + 3 * k + c] = y
+        v, own, py_, pz_ = [[early[6 + 3 * k + c] for c in range(3)] for k in range(4)]
+        if corners:
+            at_edge = jnp.logical_and(jnp.logical_and(sub == 0, in8 < 2), down[1])
+            corner = split([d_xpym[r, h] for h in range(2)])[1:]
+            py_ = [jnp.where(at_edge, corner[c], py_[c]) for c in range(3)]
+        new = q_step([qux[i] for i in range(6)], v, [own, py_, pz_])
         if corners:
             for i in range(6):
                 qux[i] = new[i]
@@ -627,7 +638,7 @@
         out_specs=(here,) * 6,
         scratch_shapes=[
             vmem(4, NZ + 2, ROWS, NX), vmem(4, NZ + 2, ROWS, NX), vmem(4, NZ + 2, ROWS, NX),
-            vmem(ITERS, 2, *tile), vmem(ITERS, 2, 2, *tile), vmem(2, *tile), vmem(13, *tile),
+            vmem(ITERS, 2, *tile), vmem(ITERS, 2, 2, *tile), vmem(2, *tile), vmem(13, *tile), vmem(18, *tile),
             vmem(ITERS, 2, *tile), vmem(ITERS, 2, *tile),
             vmem(ITERS, 2, *tile), vmem(ITERS, 2, *tile), vmem(ITERS, 2, *tile), vmem(ITERS, 2, *tile),
             vmem(2, *tile), vmem(3, *tile), vmem(3, *tile), vmem(6, *tile), vmem(3, NY, NX), vmem(6, NY, NX),

time: 23 us -> 22.9 us (level)
  no operation moved by 1% of the time
where the time goes in v6:
time: 22.9 us; the launch traced here: 22.7 us
  Pallas kernels  22.1 us (97%)
  between operations  0.64 us (3%)
    pallas_call x1, Pallas kernels, per_device(): pl.pallas_call(functools.partial(exchange_kernel, sizes), out_shape=(vmem...  20.9 us
    pallas_call x1, Pallas kernels, per_device(): pl.pallas_call(functools.partial(final_kernel, sizes), out_shape=tuple((j...  1.24 us

profile of v6, /device:TPU:7, one launch (start us, length us, event | category | flops | bytes accessed | tf_op | source)
XLA Modules:
  0.0 22.7 jit_solution(5612409124269548368)
XLA Ops:
  0.6 20.9 %tgv_rounds.1 = (f32[4,8,32,128]{3,2,1,0:T(8,128)S(1)}, f32[3,9,40,128]{3,2,1,0:T(8,128)S(1)}, f32[6,9,40,128]{3,2,1,0:T(8,128)S(1)}, f32[8,32,128]{2,1,0:T(8,12...) custom-call(f32[8,32,128]{2,1,0:T(8,128)} %f_in.1, f32[8,32,128]{2,1,0:T(8,128)} %w_in.1, ...), custom_call_target="tpu_custom_call" | custom-call | tf_op jit(solution)/shard_map/tgv_rounds/pallas_call | solution.py:627
  21.5 1.2 %tgv_last.1 = (f32[8,32,128]{2,1,0:T(8,128)}, f32[3,8,32,128]{3,2,1,0:T(8,128)}, f32[3,8,32,128]{3,2,1,0:T(8,128)}, f32[6,8,32,128]{3,2,1,0:T(8,128)}) custom-call(f32[4,8,32,128]{3,2,1,0:T(8,128)S(1)} %get-tuple-element.10.uv, f32[3,9,40,128]{3,2,1,0:T(8,128)S(1)} %get-tuple-element.11.p, f32[6,9,40,128]{3,2,1,0:T(8,128)S(1)} %get-tuple-element.12.q, ...), custom_call_target="tpu_custom_call" | custom-call | tf_op jit(solution)/shard_map/tgv_last/pallas_call | solution.py:656
